TPU v7x, 1024 devices: a whole 4x8x16 slice. The times are simulated.
1024 devices in a mesh: dp: 16 (over y, core), expert: 64 (over z, x).
Axes of the slice: x: 4, y: 8, z: 16, core: 2. Of those that a mesh axis runs over, the one named last changes fastest.
Arguments:
- tokens: bfloat16 [16, 8192, 4096], P('dp', 'expert'), may hold values from -20 to 20
- router_weight: bfloat16 [4096, 128], replicated
- chosen: int32 [16, 8, 128], P('dp'), may hold values from 0 to 8191, as said below
- w_gate: bfloat16 [4096, 12288], P(None, 'expert'), may hold values from -0.09375 to 0.09375
- w_up: bfloat16 [4096, 12288], P(None, 'expert'), may hold values from -0.09375 to 0.09375
- w_down: bfloat16 [12288, 4096], P('expert'), may hold values from -0.15625 to 0.15625
Outputs:
- combined: bfloat16 [16, 8192, 4096], P('dp', 'expert')
- z_loss: float32 [], replicated
Inputs may be any that keep to these rules, and one draw needn't show every extreme that they name: Each list chosen[g, e] holds 128 distinct positions of window g; at most 4 of them lie in any one aligned block of 128 positions (the tokens of one device), and some block holds exactly 4.
All inputs are finite; a program needn't handle non-finite values.
Results may differ from a plain program's by a relative error of at most 0.009.
Values may be sent and summed in bfloat16 or wider, within the bound.
No kernel may reach another device: no remote copies, remote signals or barrier semaphores. Data moves between devices by JAX's collectives and lax.ppermute only.
A program may use at most 64 MiB of HBM per device.

v0:
```python
import jax
import jax.numpy as jnp
from jax import lax
from jax.sharding import Mesh
from jax.sharding import PartitionSpec as P

EXPERT = ("expert_0", "expert_1")
DP_EXPERT = ("dp_0", "dp_1", "expert_0", "expert_1")
DP = ("dp_0", "dp_1")


def by_axis(shard, axes):
    for axis in axes:
        shard = lax.psum(shard, axis)
    return shard


def partner_2(value, axis, stride):
    mask = 2**stride
    pairs = [(source, source ^ mask) for source in range(lax.axis_size(axis))]
    return lax.ppermute(value, axis, pairs)


def block_index(device, bit_list):
    levels = len(bit_list)
    block_sum = jnp.zeros_like(device)
    for position, bit_no in enumerate(bit_list):
        block_sum = block_sum + (device >> bit_no & 1) * (1 << levels - 1 - position)
    return block_sum


def body(tokens, router_weight, chosen, w_gate, w_up, w_down):
    token_rows = tokens[0]
    picked = chosen[0]
    experts_here = picked.shape[0]
    rows_dev = token_rows.shape[0]
    width = token_rows.shape[1]
    devices = lax.axis_size(EXPERT)
    split = devices // experts_here
    levels = split.bit_length() - 1
    most = 2 * picked.shape[1] // devices
    piece_width = width // split
    my_index = lax.axis_index(EXPERT)
    bit_list = list(range(levels))
    logits = jnp.dot(token_rows, router_weight, preferred_element_type=jnp.float32)
    highest = jnp.max(logits, axis=1, keepdims=True)
    log_total = highest[:, 0] + jnp.log(jnp.sum(jnp.exp(logits - highest), axis=1))
    loss_total = by_axis(jnp.sum(log_total * log_total), DP_EXPERT)
    z_loss = loss_total / (lax.axis_size(DP) * devices * rows_dev)
    local_pos = picked - my_index * rows_dev
    inside = (local_pos >= 0) & (local_pos < rows_dev)
    inside_int = inside.astype(jnp.int32)
    rank = jnp.cumsum(inside_int, axis=1) - inside_int
    slot = jnp.where(inside, rank, most)
    expert_ids = jnp.arange(experts_here, dtype=jnp.int32)[:, None]
    slot_token = (
        jnp.full((experts_here, most), rows_dev, jnp.int32)
        .at[expert_ids, slot]
        .set(local_pos, mode="drop")
    )
    member = jnp.any(
        local_pos[:, :, None] == jnp.arange(rows_dev, dtype=jnp.int32)[None, None, :], axis=1
    ).T
    window = logits[:, :experts_here]
    peak = jnp.max(jnp.where(member, window, -1e30), axis=1, keepdims=True)
    peak = jnp.where(jnp.any(member, axis=1, keepdims=True), peak, 0.0)
    raised = jnp.where(member, jnp.exp(jnp.where(member, window - peak, -60.0)), 0.0)
    denom = jnp.sum(raised, axis=1, keepdims=True)
    combine = raised / jnp.where(denom > 0, denom, 1.0)
    combine_pad = jnp.concatenate([combine, jnp.zeros((1, experts_here), jnp.float32)], axis=0)
    slot_weight = combine_pad[slot_token, expert_ids]
    rows_pad = jnp.concatenate([token_rows, jnp.zeros((1, width), token_rows.dtype)], axis=0)
    slot_rows = rows_pad[slot_token]
    device_ids = jnp.arange(split, dtype=jnp.int32)
    blocks = block_index(device_ids, bit_list)
    inverse = jnp.argsort(blocks)
    pieces = slot_rows.reshape(experts_here, most, split, piece_width)
    pieces = jnp.take(pieces, blocks, axis=2)
    outgoing = pieces.transpose(0, 2, 1, 3).reshape(devices, most, piece_width)
    arrived = lax.all_to_all(outgoing, EXPERT, split_axis=0, concat_axis=0, tiled=True)
    for bit_no in reversed(bit_list):
        partner = partner_2(arrived, EXPERT, bit_no)
        lower_side = my_index >> bit_no & 1 == 0
        arrived = jnp.where(
            lower_side,
            jnp.concatenate([arrived, partner], axis=2),
            jnp.concatenate([partner, arrived], axis=2),
        )
    flat_rows = arrived.reshape(devices * most, width)
    gate = jnp.dot(flat_rows, w_gate, preferred_element_type=jnp.float32)
    upper = jnp.dot(flat_rows, w_up, preferred_element_type=jnp.float32)
    hidden = (jax.nn.silu(gate) * upper).astype(jnp.bfloat16)
    rounded = (
        jnp.dot(hidden, w_down, preferred_element_type=jnp.float32)
        .astype(jnp.bfloat16)
        .reshape(devices, most, width)
    )
    held = rounded.reshape(devices, most, 1, width)
    for bit_no in bit_list:
        half_width = held.shape[3] // 2
        lower_half = held[:, :, :, :half_width]
        upper_half = held[:, :, :, half_width:]
        lower_side = my_index >> bit_no & 1 == 0
        keeping = jnp.where(lower_side, lower_half, upper_half)
        sending = jnp.where(lower_side, upper_half, lower_half)
        received = partner_2(sending, EXPERT, bit_no)
        held = jnp.concatenate([keeping, received], axis=2)
    expert_out = jnp.sum(held.astype(jnp.float32), axis=2).astype(jnp.bfloat16)
    returned = lax.all_to_all(expert_out, EXPERT, split_axis=0, concat_axis=0, tiled=True)
    returned = jnp.take(returned.reshape(experts_here, split, most, piece_width), inverse, axis=1)
    full_out = returned.transpose(0, 2, 1, 3).reshape(experts_here, most, width)
    contrib = slot_weight[:, :, None] * full_out.astype(jnp.float32)
    mixed = (
        jnp.zeros((rows_dev, width), jnp.float32)
        .at[slot_token.reshape(-1)]
        .add(contrib.reshape(-1, width), mode="drop")
    )
    return (mixed.astype(jnp.bfloat16)[None], z_loss)


def solution(mesh):
    split = Mesh(mesh.devices.reshape(8, 2, 16, 4), ("dp_0", "dp_1", "expert_0", "expert_1"))
    in_specs = (
        P(DP, EXPERT, None),
        P(),
        P(DP, None, None),
        P(None, EXPERT),
        P(None, EXPERT),
        P(EXPERT, None),
    )
    out_specs = (P(DP, EXPERT, None), P())
    return jax.shard_map(body, mesh=split, in_specs=in_specs, out_specs=out_specs, check_vma=False)
```

profile of v0, /device:TPU:2, one launch (start us, length us, event | category | flops | bytes accessed | tf_op | source)
XLA Modules:
  0.0 263.9 jit_solution(11928467893614449706)
XLA Ops:
  4.6 4.3 %scatter_custom_fusion.1 = s32[32]{0:T(128)S(1)} fusion(s32[1024]{0:T(1024)S(1)} %bitcast.60, s32[1024]{0:T(1024)S(1)} %get-tuple-element.13, s32[]{:T(128)} %constant.22.clone.1), kind=kCustom, calls=%fused_computation.92 | custom fusion | bytes 132
  12.5 43.6 %all_to_all.10 = bf16[64,4,512]{2,1,0:T(4,128)(2,1)S(1)} all-to-all(bf16[64,4,512]{2,1,0:T(4,128)(2,1)S(1)} %copy.73), channel_id=1, replica_groups=mesh['dp_0'=8,'dp_1'=2,'expert_0'=16,'expert_1'=4] {'expert_0','expert_1'}, dimensions={0} | all-to-all | bytes 524288 | tf_op jit(solution)/shard_map/all_to_all | solution.py:80
  56.2 3.0 %collective-permute-start = (bf16[64,4,512]{2,1,0:T(4,128)(2,1)S(1)}, bf16[64,4,512]{2,1,0:T(4,128)(2,1)S(1)}, u32[]{:S(2)}, u32[]{:S(2)}) collective-permute-start(bf16[64,4,512]{2,1,0:T(4,128)(2,1)S(1)} %all_to_all.10), channel_id=1, source_target_pairs={{0,4},{1,5},{2,6},{3,7},{4,0},{5,1},{6,2},{7,3},{8,12},{9,13},{10,... | collective-permute-start | bytes 786440 | tf_op jit(solution)/shard_map/ppermute | solution.py:21
  59.2 5.2 %collective-permute-done = bf16[64,4,512]{2,1,0:T(4,128)(2,1)S(1)} collective-permute-done((bf16[64,4,512]{2,1,0:T(4,128)(2,1)S(1)}, bf16[64,4,512]{2,1,0:T(4,128)(2,1)S(1)}, u32[]{:S(2)}, u32[]{:S(2)}) %collective-permute-start) | collective-permute-done | bytes 262176 | tf_op jit(solution)/shard_map/ppermute | solution.py:21
  64.8 3.9 %collective-permute-start.1 = (bf16[64,4,1024]{2,1,0:T(4,128)(2,1)S(1)}, bf16[64,4,1024]{2,1,0:T(4,128)(2,1)S(1)}, u32[]{:S(2)}, u32[]{:S(2)}) collective-permute-start(bf16[64,4,1024]{2,1,0:T(4,128)(2,1)S(1)} %maximum_select_fusion.4), channel_id=1, source_target_pairs={{0,2},{1,3},{2,0},{3,1},{4,6},{5,7},{6,4},{7,5},{8,10},{9,11},{10,... | collective-permute-start | bytes 1572872 | tf_op jit(solution)/shard_map/ppermute | solution.py:21
  68.8 10.0 %collective-permute-done.1 = bf16[64,4,1024]{2,1,0:T(4,128)(2,1)S(1)} collective-permute-done((bf16[64,4,1024]{2,1,0:T(4,128)(2,1)S(1)}, bf16[64,4,1024]{2,1,0:T(4,128)(2,1)S(1)}, u32[]{:S(2)}, u32[]{:S(2)}) %collective-permute-start.1) | collective-permute-done | bytes 524320 | tf_op jit(solution)/shard_map/ppermute | solution.py:21
  84.4 19.3 %collective-permute-done.2 = bf16[64,4,2048]{2,1,0:T(4,128)(2,1)} collective-permute-done((bf16[64,4,2048]{2,1,0:T(4,128)(2,1)}, bf16[64,4,2048]{2,1,0:T(4,128)(2,1)}, u32[]{:S(2)}, u32[]{:S(2)}) %collective-permute-start.2) | collective-permute-done | bytes 1048608 | tf_op jit(solution)/shard_map/ppermute | solution.py:21
  105.9 2.9 %fusion.11 = f32[256,192]{0,1:T(8,128)S(1)} fusion(bf16[4096,192]{0,1:T(8,128)(2,1)} %param.10, bf16[256,2048]{1,0:T(8,128)(2,1)} %concatenate.74, bf16[256,2048]{1,0:T(8,128)(2,1)S(1)} %copy-done.3, pred[]{:T(512)S(6)} %eq.30), kind=kOutput, calls=%fused_computation.38 | convolution fusion | flops 412090368 | bytes 3866625 | tf_op jit(solution)/shard_map/dot_general | solution.py:91
  108.8 6.0 %convolution_convert_fusion = bf16[256,4096]{1,0:T(8,128)(2,1)} fusion(bf16[192,4096]{1,0:T(8,128)(2,1)S(1)} %copy-done, f32[256,192]{0,1:T(8,128)S(1)} %fusion.11, bf16[4096,192]{0,1:T(8,128)(2,1)} %param.9, bf16[256,2048]{1,0:T(8,128)(2,1)} %concatenate.74, bf16[256,2048]{1,0:T(8,128)(2,1)S(1)} %copy-done.3, pred[]{:T(512)S(6)} %eq.30), kind=kOutput, calls=%fused_computation.6 | convolution fusion | flops 816087040 | bytes 7536641 | tf_op jit(solution)/shard_map/dot_general | solution.py:94
  114.7 4.1 %reshape_reshape.3 = bf16[64,4,1,4096]{3,1,0,2:T(4,128)(2,1)} reshape(bf16[256,4096]{1,0:T(8,128)(2,1)} %convolution_convert_fusion) | data formatting | bytes 4194304 | tf_op jit(solution)/shard_map/reshape;reshape | solution.py:98
  118.9 2.4 broadcast_select_fusion.1
  121.3 2.2 collective-permute-start.3
  123.5 19.8 %collective-permute-done.3 = bf16[64,4,1,2048]{3,1,0,2:T(4,128)(2,1)S(1)} collective-permute-done((bf16[64,4,1,2048]{3,1,0,2:T(4,128)(2,1)S(1)}, bf16[64,4,1,2048]{3,1,0,2:T(4,128)(2,1)S(1)}, u32[]{:S(2)}, u32[]{:S(2)}) %collective-permute-start.3) | collective-permute-done | bytes 1048608 | tf_op jit(solution)/shard_map/ppermute | solution.py:21
  145.3 4.0 %collective-permute-start.4 = (bf16[64,4,2,1024]{3,1,0,2:T(4,128)(2,1)}, bf16[64,4,2,1024]{3,1,0,2:T(4,128)(2,1)}, u32[]{:S(2)}, u32[]{:S(2)}) collective-permute-start(bf16[64,4,2,1024]{3,1,0,2:T(4,128)(2,1)} %get-tuple-element.9), channel_id=1, source_target_pairs={{0,2},{1,3},{2,0},{3,1},{4,6},{5,7},{6,4},{7,5},{8,10},{9,11},{10,... | collective-permute-start | bytes 3145736 | tf_op jit(solution)/shard_map/ppermute | solution.py:21
  150.5 18.2 %psum.28 = f32[]{:T(128)} all-reduce(f32[]{:T(128)} %multiply_reduce_fusion.1), channel_id=1, replica_groups=mesh['dp_0'=8,'dp_1'=2,'expert_0'=16,'expert_1'=4] {'dp_0'}, use_global_device_ids=true, to_apply=%region_13.14 | all-reduce | flops 1 | bytes 8 | tf_op jit(solution)/shard_map/psum | solution.py:14
  168.7 3.1 %psum.29 = f32[]{:T(128)} all-reduce(f32[]{:T(128)} %psum.28), channel_id=1, replica_groups=mesh['dp_0'=8,'dp_1'=2,'expert_0'=16,'expert_1'=4] {'dp_1'}, use_global_device_ids=true, to_apply=%region_14.15 | all-reduce | flops 1 | bytes 8 | tf_op jit(solution)/shard_map/psum | solution.py:14
  171.8 31.9 %psum.30 = f32[]{:T(128)} all-reduce(f32[]{:T(128)} %psum.29), channel_id=1, replica_groups=mesh['dp_0'=8,'dp_1'=2,'expert_0'=16,'expert_1'=4] {'expert_0'}, use_global_device_ids=true, to_apply=%region_15.16 | all-reduce | flops 1 | bytes 8 | tf_op jit(solution)/shard_map/psum | solution.py:14
  206.0 3.9 %collective-permute-start.5 = (bf16[64,4,4,512]{3,1,0,2:T(4,128)(2,1)S(1)}, bf16[64,4,4,512]{3,1,0,2:T(4,128)(2,1)}, u32[]{:S(2)}, u32[]{:S(2)}) collective-permute-start(bf16[64,4,4,512]{3,1,0,2:T(4,128)(2,1)S(1)} %get-tuple-element.6), channel_id=1, source_target_pairs={{0,4},{1,5},{2,6},{3,7},{4,0},{5,1},{6,2},{7,3},{8,12},{9,13},{10,... | collective-permute-start | bytes 3145736 | tf_op jit(solution)/shard_map/ppermute | solution.py:21
  212.1 14.3 %collective-permute-done.5 = bf16[64,4,4,512]{3,1,0,2:T(4,128)(2,1)} collective-permute-done((bf16[64,4,4,512]{3,1,0,2:T(4,128)(2,1)S(1)}, bf16[64,4,4,512]{3,1,0,2:T(4,128)(2,1)}, u32[]{:S(2)}, u32[]{:S(2)}) %collective-permute-start.5) | collective-permute-done | bytes 1048608 | tf_op jit(solution)/shard_map/ppermute | solution.py:21
  229.1 8.9 %all-to-all-start.1 = ((bf16[64,4,512]{2,1,0:T(4,128)(2,1)}), bf16[64,4,512]{2,1,0:T(4,128)(2,1)S(1)}, u32[]{:S(2)}, u32[]{:S(2)}) async-start(bf16[64,4,512]{2,1,0:T(4,128)(2,1)} %reduce_sum.50), calls=%async_computation.1 | async-start | bytes 524288 | tf_op jit(solution)/shard_map/all_to_all | solution.py:109
  238.0 9.3 %psum.31 = f32[]{:T(128)} all-reduce(f32[]{:T(128)} %psum.30), channel_id=1, replica_groups=mesh['dp_0'=8,'dp_1'=2,'expert_0'=16,'expert_1'=4] {'expert_1'}, use_global_device_ids=true, to_apply=%region_16.17 | all-reduce | flops 1 | bytes 8 | tf_op jit(solution)/shard_map/psum | solution.py:14
  250.1 5.8 %all-to-all-done.1 = bf16[64,4,512]{2,1,0:T(4,128)(2,1)S(1)} async-done(((bf16[64,4,512]{2,1,0:T(4,128)(2,1)}), bf16[64,4,512]{2,1,0:T(4,128)(2,1)S(1)}, u32[]{:S(2)}, u32[]{:S(2)}) %all-to-all-start.1) | async-done | bytes 262176 | tf_op jit(solution)/shard_map/all_to_all | solution.py:109
  257.3 2.8 %scatter_custom_fusion = f32[128,4096]{1,0:T(8,128)} fusion(s32[32]{0:T(128)S(1)} %fusion.32, f32[]{:T(128)} %constant.21.clone.1, f32[32,4096]{1,0:T(8,128)S(1)} %bitcast.53, f32[32]{0:T(128)S(1)} %gather_fusion), kind=kCustom, calls=%fused_computation.21 | custom fusion | flops 262144 | bytes 2621956 | tf_op jit(solution)/shard_map/scatter-add | solution.py:116
  260.1 2.7 %convert_bitcast_fusion = bf16[1,128,4096]{2,1,0:T(8,128)(2,1)} fusion(f32[128,4096]{1,0:T(8,128)} %scatter_custom_fusion), kind=kLoop, calls=%fused_computation.19 | loop fusion | flops 524288 | bytes 3145728 | tf_op jit(solution)/shard_map/broadcast_in_dim | solution.py:118
  (79 shorter events, 29.4 us)
Async XLA Ops:
  0.6 108.1 %copy-start = (bf16[192,4096]{1,0:T(8,128)(2,1)S(1)}, bf16[192,4096]{1,0:T(8,128)(2,1)}, u32[]{:S(2)}) copy-start(bf16[192,4096]{1,0:T(8,128)(2,1)} %param.11) | copy-start | bytes 4718596
  56.2 8.3 %collective-permute-start = (bf16[64,4,512]{2,1,0:T(4,128)(2,1)S(1)}, bf16[64,4,512]{2,1,0:T(4,128)(2,1)S(1)}, u32[]{:S(2)}, u32[]{:S(2)}) collective-permute-start(bf16[64,4,512]{2,1,0:T(4,128)(2,1)S(1)} %all_to_all.10), channel_id=1, source_target_pairs={{0,4},{1,5},{2,6},{3,7},{4,0},{5,1},{6,2},{7,3},{8,12},{9,13},{10,... | collective-permute-start | bytes 786440 | tf_op jit(solution)/shard_map/ppermute | solution.py:21
  64.8 14.0 %collective-permute-start.1 = (bf16[64,4,1024]{2,1,0:T(4,128)(2,1)S(1)}, bf16[64,4,1024]{2,1,0:T(4,128)(2,1)S(1)}, u32[]{:S(2)}, u32[]{:S(2)}) collective-permute-start(bf16[64,4,1024]{2,1,0:T(4,128)(2,1)S(1)} %maximum_select_fusion.4), channel_id=1, source_target_pairs={{0,2},{1,3},{2,0},{3,1},{4,6},{5,7},{6,4},{7,5},{8,10},{9,11},{10,... | collective-permute-start | bytes 1572872 | tf_op jit(solution)/shard_map/ppermute | solution.py:21
  80.6 23.1 %collective-permute-start.2 = (bf16[64,4,2048]{2,1,0:T(4,128)(2,1)}, bf16[64,4,2048]{2,1,0:T(4,128)(2,1)}, u32[]{:S(2)}, u32[]{:S(2)}) collective-permute-start(bf16[64,4,2048]{2,1,0:T(4,128)(2,1)} %maximum_select_fusion.2), channel_id=1, source_target_pairs={{0,1},{1,0},{2,3},{3,2},{4,5},{5,4},{6,7},{7,6},{8,9},{9,8},{10,11... | collective-permute-start | bytes 3145736 | tf_op jit(solution)/shard_map/ppermute | solution.py:21
  84.4 21.5 %copy-start.3 = (bf16[256,2048]{1,0:T(8,128)(2,1)S(1)}, bf16[256,2048]{1,0:T(8,128)(2,1)}, u32[]{:S(2)}) copy-start(bf16[256,2048]{1,0:T(8,128)(2,1)} %maximum_select_fusion.1) | copy-start | bytes 3145732
  121.3 22.0 %collective-permute-start.3 = (bf16[64,4,1,2048]{3,1,0,2:T(4,128)(2,1)S(1)}, bf16[64,4,1,2048]{3,1,0,2:T(4,128)(2,1)S(1)}, u32[]{:S(2)}, u32[]{:S(2)}) collective-permute-start(bf16[64,4,1,2048]{3,1,0,2:T(4,128)(2,1)S(1)} %get-tuple-element.11), channel_id=1, source_target_pairs={{0,1},{1,0},{2,3},{3,2},{4,5},{5,4},{6,7},{7,6},{8,9},{9,8},{10,11... | collective-permute-start | bytes 3145736 | tf_op jit(solution)/shard_map/ppermute | solution.py:21
  143.3 6.0 %copy-start.1 = (bf16[1,128,4096]{2,1,0:T(8,128)(2,1)S(1)}, bf16[1,128,4096]{2,1,0:T(8,128)(2,1)}, u32[]{:S(2)}) copy-start(bf16[1,128,4096]{2,1,0:T(8,128)(2,1)} %param.6) | copy-start | bytes 3145732
  143.3 6.0 %copy-start.2 = (bf16[4096,128]{1,0:T(8,128)(2,1)S(1)}, bf16[4096,128]{1,0:T(8,128)(2,1)}, u32[]{:S(2)}) copy-start(bf16[4096,128]{1,0:T(8,128)(2,1)} %param.7) | copy-start | bytes 3145732
  145.3 58.6 %collective-permute-start.4 = (bf16[64,4,2,1024]{3,1,0,2:T(4,128)(2,1)}, bf16[64,4,2,1024]{3,1,0,2:T(4,128)(2,1)}, u32[]{:S(2)}, u32[]{:S(2)}) collective-permute-start(bf16[64,4,2,1024]{3,1,0,2:T(4,128)(2,1)} %get-tuple-element.9), channel_id=1, source_target_pairs={{0,2},{1,3},{2,0},{3,1},{4,6},{5,7},{6,4},{7,5},{8,10},{9,11},{10,... | collective-permute-start | bytes 3145736 | tf_op jit(solution)/shard_map/ppermute | solution.py:21
  206.0 20.4 %collective-permute-start.5 = (bf16[64,4,4,512]{3,1,0,2:T(4,128)(2,1)S(1)}, bf16[64,4,4,512]{3,1,0,2:T(4,128)(2,1)}, u32[]{:S(2)}, u32[]{:S(2)}) collective-permute-start(bf16[64,4,4,512]{3,1,0,2:T(4,128)(2,1)S(1)} %get-tuple-element.6), channel_id=1, source_target_pairs={{0,4},{1,5},{2,6},{3,7},{4,0},{5,1},{6,2},{7,3},{8,12},{9,13},{10,... | collective-permute-start | bytes 3145736 | tf_op jit(solution)/shard_map/ppermute | solution.py:21
  229.1 26.7 %all-to-all-start.1 = ((bf16[64,4,512]{2,1,0:T(4,128)(2,1)}), bf16[64,4,512]{2,1,0:T(4,128)(2,1)S(1)}, u32[]{:S(2)}, u32[]{:S(2)}) async-start(bf16[64,4,512]{2,1,0:T(4,128)(2,1)} %reduce_sum.50), calls=%async_computation.1 | async-start | bytes 524288 | tf_op jit(solution)/shard_map/all_to_all | solution.py:109
where the time goes:
time: 265 us; the launch traced here: 264 us
  blocking collectives  106 us (40%)
  waiting for transfers between devices  74.4 us (28%)
  starting transfers between devices  27.9 us (11%)
  other arithmetic  25.9 us (10%)
  local copies, waits for them, and re-layouts  17.4 us (7%)
  matrix products  9.39 us (4%)
  between operations  2.82 us (1%)
    ppermute x6, waiting for transfers between devices, partner_2(): return lax.ppermute(value, axis, pairs)  68.7 us
    psum x4, blocking collectives, by_axis(): shard = lax.psum(shard, axis)  62.5 us
    all_to_all x1, blocking collectives, body(): lax.all_to_all(outgoing, EXPERT, split_axis=0, concat_axis=0, tiled=True)  43.6 us
    ppermute x6, starting transfers between devices, partner_2(): return lax.ppermute(value, axis, pairs)  19 us
    all_to_all x1, starting transfers between devices, body(): lax.all_to_all(expert_out, EXPERT, split_axis=0, concat_axis=0, tiled=True)  8.87 us
    dot_general x1, matrix products, body(): jnp.dot(hidden, w_down, preferred_element_type=jnp.float32)  5.96 us
    all_to_all x1, waiting for transfers between devices, body(): lax.all_to_all(expert_out, EXPERT, split_axis=0, concat_axis=0, tiled=True)  5.77 us
  transfers between devices with their start and end apart: 7, of which 6 were waited for; matrix products, arithmetic and copies ran while one was open for 3% of the time, Pallas kernels for 0%

commit v1 on v0

v1 whole, which is shorter than its diff:
```python
import jax
import jax.numpy as jnp
from jax import lax
from jax.sharding import Mesh
from jax.sharding import PartitionSpec as P


DP = ("dp_0", "dp_1")
EXPERT = ("ez", "zp", "x")
SHARE = ("zp", "x")
LANES = 128


def three_terms(value):
    high = value.astype(jnp.bfloat16)
    left = value - high.astype(jnp.float32)
    middle = left.astype(jnp.bfloat16)
    low = (left - middle.astype(jnp.float32)).astype(jnp.bfloat16)
    return jnp.stack([high, middle, low])


def exchange_down(w_down, zp, x, n_zp, n_x, piece):
    rows = w_down.shape[0]
    half = n_x * piece
    other = lax.dynamic_slice(w_down, (0, (1 - zp) * half), (rows, half))
    other = lax.ppermute(other, "zp", [(i, 1 - i) for i in range(n_zp)])
    down = jnp.zeros((n_zp, n_x, rows, piece), w_down.dtype)
    for step in range(n_x):
        block = (x + step) % n_x * piece
        own_part = lax.dynamic_slice(w_down, (0, zp * half + block), (rows, piece))
        part = jnp.stack([own_part, lax.dynamic_slice(other, (0, block), (rows, piece))])
        if step:
            part = lax.ppermute(part, "x", [(i, (i + step) % n_x) for i in range(n_x)])
        source = (x + n_x - step) % n_x
        down = lax.dynamic_update_slice(down, part[0][None, None], (zp, source, 0, 0))
        down = lax.dynamic_update_slice(down, part[1][None, None], (1 - zp, source, 0, 0))
    return down.reshape(n_zp * n_x, rows, piece)


def copy_to(value, axes, count):
    return lax.all_to_all(jnp.broadcast_to(value[None], (count,) + value.shape), axes, 0, 0, tiled=True)


def layer(tokens, router_weight, chosen, w_gate, w_up, w_down):
    token_rows = tokens[0]
    picked = chosen[0]
    experts, cap = picked.shape
    rows_dev, width = token_rows.shape
    devices = lax.axis_size(EXPERT)
    n_dp = lax.axis_size(DP)
    n_zp = lax.axis_size("zp")
    n_x = lax.axis_size("x")
    split = n_zp * n_x
    most = 2 * cap // devices
    piece = width // split
    hidden_cols = w_gate.shape[1]
    me = lax.axis_index(EXPERT)

    local_pos = picked - me * rows_dev
    token_ids = jnp.arange(rows_dev, dtype=jnp.int32)
    member = jnp.any(local_pos[:, :, None] == token_ids[None, None, :], axis=1)
    before = (token_ids[:, None] < token_ids[None, :]).astype(jnp.bfloat16)
    rank = jnp.dot(member.astype(jnp.bfloat16), before, preferred_element_type=jnp.float32)
    slots = jnp.arange(most, dtype=jnp.float32)
    taken = member[:, None, :] & (rank[:, None, :] == slots[None, :, None])
    pick_mat = taken.reshape(experts * most, rows_dev).astype(jnp.bfloat16)
    slot_rows = jnp.dot(pick_mat, token_rows, preferred_element_type=jnp.float32).astype(jnp.bfloat16)
    outgoing = slot_rows.reshape(experts, most, split, piece).transpose(0, 2, 1, 3).reshape(devices, most, piece)
    outgoing, logit_rows, member, taken = lax.optimization_barrier((outgoing, token_rows, member, taken))
    arrived = lax.all_to_all(outgoing, EXPERT, 0, 0, tiled=True)

    down = exchange_down(w_down, lax.axis_index("zp"), lax.axis_index("x"), n_zp, n_x, piece)

    mine = lax.dynamic_index_in_dim(picked, lax.axis_index("ez"), 0, keepdims=False)
    owner = mine // rows_dev
    device_ids = jnp.arange(devices, dtype=jnp.int32)
    first = jnp.sum((owner[None, :] < device_ids[:, None]).astype(jnp.int32), axis=1)
    count = jnp.sum((owner[None, :] == device_ids[:, None]).astype(jnp.int32), axis=1)
    slot_ids = jnp.arange(most, dtype=jnp.int32)[None, :]
    target = jnp.where(slot_ids < count[:, None], first[:, None] + slot_ids, -1).reshape(-1)
    pack_mat = (jnp.arange(cap, dtype=jnp.int32)[:, None] == target[None, :]).astype(jnp.bfloat16)
    packed = jnp.dot(
        pack_mat, arrived.reshape(devices * most, piece), preferred_element_type=jnp.float32
    ).astype(jnp.bfloat16)

    rows = copy_to(packed, SHARE, split)
    gate = jnp.einsum("kpd,kdf->pf", rows, w_gate.reshape(split, piece, hidden_cols), preferred_element_type=jnp.float32)
    upper = jnp.einsum("kpd,kdf->pf", rows, w_up.reshape(split, piece, hidden_cols), preferred_element_type=jnp.float32)
    hidden = (jax.nn.silu(gate) * upper).astype(jnp.bfloat16)
    hidden = copy_to(hidden, SHARE, split)
    expert_out = jnp.einsum("kpf,kfd->pd", hidden, down, preferred_element_type=jnp.float32).astype(jnp.bfloat16)
    spread = lax.dot_general(
        pack_mat, expert_out, (((0,), (0,)), ((), ())), preferred_element_type=jnp.float32
    ).astype(jnp.bfloat16)

    logits = jnp.dot(logit_rows, router_weight, preferred_element_type=jnp.float32)
    highest = jnp.max(logits, axis=1, keepdims=True)
    log_total = highest[:, 0] + jnp.log(jnp.sum(jnp.exp(logits - highest), axis=1))
    loss = jnp.sum(log_total * log_total)
    loss = lax.psum(loss, "dp_1")
    loss = lax.psum(loss, "dp_0")

    terms = jnp.pad(three_terms(loss), (0, LANES - 3))
    terms = jnp.broadcast_to(terms[None, None, :], (devices, most, LANES))
    returned = jnp.concatenate([spread.reshape(devices, most, piece), terms], axis=2)
    returned = lax.all_to_all(returned, EXPERT, 0, 0, tiled=True)
    loss = jnp.sum(returned[:, 0, piece:].astype(jnp.float32))
    z_loss = loss / (n_dp * devices * rows_dev)
    full_out = (
        returned[:, :, :piece].reshape(experts, split, most, piece).transpose(0, 2, 1, 3).reshape(experts * most, width)
    )

    window = logits[:, :experts].T
    peak = jnp.max(jnp.where(member, window, -1e30), axis=0, keepdims=True)
    peak = jnp.where(jnp.any(member, axis=0, keepdims=True), peak, 0.0)
    raised = jnp.where(member, jnp.exp(jnp.where(member, window - peak, -60.0)), 0.0)
    denom = jnp.sum(raised, axis=0, keepdims=True)
    combine = raised / jnp.where(denom > 0, denom, 1.0)
    weights = jnp.where(taken, combine[:, None, :], 0.0).reshape(experts * most, rows_dev)
    coarse = weights.astype(jnp.bfloat16)
    fine = (weights - coarse.astype(jnp.float32)).astype(jnp.bfloat16)
    over_slots = (((0,), (0,)), ((), ()))
    mixed = lax.dot_general(coarse, full_out, over_slots, preferred_element_type=jnp.float32)
    mixed = mixed + lax.dot_general(fine, full_out, over_slots, preferred_element_type=jnp.float32)
    return (mixed.astype(jnp.bfloat16)[None], z_loss)


def solution(mesh):
    split = Mesh(mesh.devices.reshape(8, 2, 8, 2, 4), DP + EXPERT)
    in_specs = (
        P(DP, EXPERT, None),
        P(),
        P(DP, None, None),
        P(None, EXPERT),
        P(None, EXPERT),
        P(EXPERT, None),
    )
    out_specs = (P(DP, EXPERT, None), P())
    return jax.shard_map(layer, mesh=split, in_specs=in_specs, out_specs=out_specs, check_vma=False)
```

time: 265 us -> 148 us (0.56)
  the two profiles are of different devices: /device:TPU:2 before, /device:TPU:8 now
where the time goes in v1:
time: 148 us; the launch traced here: 147 us
  starting transfers between devices  50.2 us (34%)
  waiting for transfers between devices  46.1 us (31%)
  blocking collectives  19.9 us (13%)
  local copies, waits for them, and re-layouts  12.5 us (8%)
  matrix products  7.82 us (5%)
  other arithmetic  6.66 us (4%)
  between operations  4.14 us (3%)
    all_to_all x1, waiting for transfers between devices, layer(): returned = lax.all_to_all(returned, EXPERT, 0, 0, tiled=True)  22.8 us
    all_to_all x1, starting transfers between devices, layer(): arrived = lax.all_to_all(outgoing, EXPERT, 0, 0, tiled=True)  22.2 us
    all_to_all x1, waiting for transfers between devices, layer(): arrived = lax.all_to_all(outgoing, EXPERT, 0, 0, tiled=True)  21.4 us
    psum x1, blocking collectives, layer(): loss = lax.psum(loss, 'dp_0')  16.8 us
    ppermute x3, starting transfers between devices, exchange_down(): part = lax.ppermute(part, 'x', [(i, (i + step) % n_x) for i in range(n_x)])  11.3 us
    all_to_all x2, starting transfers between devices, copy_to(): lax.all_to_all(jnp.broadcast_to(value[None], (count,) + value.shape), axe...  7.68 us
    all_to_all x1, starting transfers between devices, layer(): returned = lax.all_to_all(returned, EXPERT, 0, 0, tiled=True)  5.24 us
    dynamic_update_slice x4, local copies, waits for them, and re-layouts, exchange_down(): lax.dynamic_update_slice(down, part[0][None, None], (zp, source, 0, 0))  3.8 us
  transfers between devices with their start and end apart: 8, of which 3 were waited for; matrix products, arithmetic and copies ran while one was open for 13% of the time, Pallas kernels for 0%

profile of v1, /device:TPU:8, one launch (start us, length us, event | category | flops | bytes accessed | tf_op | source)
XLA Modules:
  0.0 147.3 jit_solution(14405592144277960818)
XLA Ops:
  3.2 22.2 %all-to-all-start = ((bf16[64,4,512]{2,1,0:T(4,128)(2,1)}), bf16[64,4,512]{2,1,0:T(4,128)(2,1)S(1)}, u32[]{:S(2)}, u32[]{:S(2)}) async-start(bf16[64,4,512]{2,1,0:T(4,128)(2,1)} %copy.26), calls=%async_computation | async-start | bytes 524288 | tf_op jit(solution)/shard_map/all_to_all | solution.py:70
  26.4 21.4 %all-to-all-done = bf16[64,4,512]{2,1,0:T(4,128)(2,1)S(1)} async-done(((bf16[64,4,512]{2,1,0:T(4,128)(2,1)}), bf16[64,4,512]{2,1,0:T(4,128)(2,1)S(1)}, u32[]{:S(2)}, u32[]{:S(2)}) %all-to-all-start) | async-done | bytes 262176 | tf_op jit(solution)/shard_map/all_to_all | solution.py:70
  48.1 1.1 broadcast_in_dim.85
  49.2 4.2 %all-to-all-start.1 = ((bf16[8,128,512]{2,1,0:T(8,128)(2,1)}), bf16[8,128,512]{2,1,0:T(8,128)(2,1)}, u32[]{:S(2)}, u32[]{:S(2)}) async-start(bf16[8,128,512]{2,1,0:T(8,128)(2,1)} %broadcast_in_dim.85), calls=%async_computation.1 | async-start | bytes 2097152 | tf_op jit(solution)/shard_map/all_to_all | solution.py:41
  53.4 1.0 constant_dynamic-slice_fusion
  54.4 3.8 %collective-permute-start = (bf16[192,2048]{1,0:T(8,128)(2,1)}, bf16[192,2048]{1,0:T(8,128)(2,1)S(1)}, u32[]{:S(2)}, u32[]{:S(2)}) collective-permute-start(bf16[192,2048]{1,0:T(8,128)(2,1)} %constant_dynamic-slice_fusion), channel_id=1, source_target_pairs={{0,4},{4,0},{1,5},{5,1},{2,6},{6,2},{3,7},{7,3},{8,12},{12,8},{9,1... | collective-permute-start | bytes 2359304 | tf_op jit(solution)/shard_map/ppermute | solution.py:26
  59.4 3.1 %psum.14 = f32[]{:T(128)} all-reduce(f32[]{:T(128)} %multiply_reduce_fusion), channel_id=1, replica_groups=mesh['dp_0'=8,'dp_1'=2,'ez'=8,'zp'=2,'x'=4] {'dp_1'}, use_global_device_ids=true, to_apply=%region_9.10 | all-reduce | flops 1 | bytes 8 | tf_op jit(solution)/shard_map/psum | solution.py:100
  62.5 16.8 %psum.15 = f32[]{:T(128)} all-reduce(f32[]{:T(128)} %psum.14), channel_id=1, replica_groups=mesh['dp_0'=8,'dp_1'=2,'ez'=8,'zp'=2,'x'=4] {'dp_0'}, use_global_device_ids=true, to_apply=%region_10.11 | all-reduce | flops 1 | bytes 8 | tf_op jit(solution)/shard_map/psum | solution.py:101
  80.9 1.0 bitcast_dynamic-update-slice_fusion.1
  81.9 1.2 dynamic-slice_bitcast_fusion.1
  83.9 3.4 %collective-permute-start.1 = (bf16[2,192,512]{2,1,0:T(8,128)(2,1)}, bf16[2,192,512]{2,1,0:T(8,128)(2,1)}, u32[]{:S(2)}, u32[]{:S(2)}) collective-permute-start(bf16[2,192,512]{2,1,0:T(8,128)(2,1)} %pad_maximum_fusion), channel_id=1, source_target_pairs={{0,1},{1,2},{2,3},{3,0},{4,5},{5,6},{6,7},{7,4},{8,9},{9,10},{10,1... | collective-permute-start | bytes 1179656 | tf_op jit(solution)/shard_map/ppermute | solution.py:33
  88.1 4.6 %collective-permute-start.2 = (bf16[2,192,512]{2,1,0:T(8,128)(2,1)}, bf16[2,192,512]{2,1,0:T(8,128)(2,1)}, u32[]{:S(2)}, u32[]{:S(2)}) collective-permute-start(bf16[2,192,512]{2,1,0:T(8,128)(2,1)} %pad_maximum_fusion.1), channel_id=1, source_target_pairs={{0,2},{1,3},{2,0},{3,1},{4,6},{5,7},{6,4},{7,5},{8,10},{9,11},{10,... | collective-permute-start | bytes 1179656 | tf_op jit(solution)/shard_map/ppermute | solution.py:33
  93.4 3.4 %collective-permute-start.3 = (bf16[2,192,512]{2,1,0:T(8,128)(2,1)}, bf16[2,192,512]{2,1,0:T(8,128)(2,1)}, u32[]{:S(2)}, u32[]{:S(2)}) collective-permute-start(bf16[2,192,512]{2,1,0:T(8,128)(2,1)} %pad_maximum_fusion.2), channel_id=1, source_target_pairs={{0,3},{1,0},{2,1},{3,2},{4,7},{5,4},{6,5},{7,6},{8,11},{9,8},{10,9... | collective-permute-start | bytes 1179656 | tf_op jit(solution)/shard_map/ppermute | solution.py:33
  96.8 2.4 %fusion.9 = f32[128,192]{0,1:T(8,128)S(1)} fusion(bf16[8,128,512]{2,1,0:T(8,128)(2,1)} %all-to-all-done.1, bf16[24,8,8,512]{3,2,1,0:T(8,128)(2,1)} %bitcast.139), kind=kOutput, calls=%fused_computation.14 | convolution fusion | flops 201326592 | bytes 2719744 | tf_op jit(solution)/shard_map/kpd,kdf->pf/dot_general | solution.py:87
  99.3 1.8 %fusion.18 = bf16[128,192]{0,1:T(8,128)(2,1)S(1)} fusion(bf16[8,128,512]{2,1,0:T(8,128)(2,1)} %all-to-all-done.1, bf16[24,8,8,512]{3,2,1,0:T(8,128)(2,1)S(1)} %bitcast.140, f32[128,192]{0,1:T(8,128)S(1)} %fusion.9), kind=kOutput, calls=%fused_computation.17 | convolution fusion | flops 201474048 | bytes 2768896 | tf_op jit(solution)/shard_map/kpd,kdf->pf/dot_general | solution.py:88
  101.9 3.5 %all-to-all-start.2 = ((bf16[8,128,192]{1,2,0:T(8,128)(2,1)}), bf16[8,128,192]{1,2,0:T(8,128)(2,1)S(1)}, u32[]{:S(2)}, u32[]{:S(2)}) async-start(bf16[8,128,192]{1,2,0:T(8,128)(2,1)} %broadcast_in_dim.86), calls=%async_computation.2 | async-start | bytes 786432 | tf_op jit(solution)/shard_map/all_to_all | solution.py:41
  106.3 0.9 fusion.26
  108.2 0.9 fusion.24
  109.2 0.9 fusion.23
  110.1 0.9 fusion.22
  111.1 1.9 %all-to-all-done.2 = bf16[8,128,192]{1,2,0:T(8,128)(2,1)S(1)} async-done(((bf16[8,128,192]{1,2,0:T(8,128)(2,1)}), bf16[8,128,192]{1,2,0:T(8,128)(2,1)S(1)}, u32[]{:S(2)}, u32[]{:S(2)}) %all-to-all-start.2) | async-done | bytes 393248 | tf_op jit(solution)/shard_map/all_to_all | solution.py:41
  114.6 5.2 %all-to-all-start.3 = ((bf16[64,4,640]{2,1,0:T(4,128)(2,1)}), bf16[64,4,640]{2,1,0:T(4,128)(2,1)S(1)}, u32[]{:S(2)}, u32[]{:S(2)}) async-start(bf16[64,4,640]{2,1,0:T(4,128)(2,1)} %pad_maximum_fusion.3), calls=%async_computation.3 | async-start | bytes 655360 | tf_op jit(solution)/shard_map/all_to_all | solution.py:106
  119.9 22.8 %all-to-all-done.3 = bf16[64,4,640]{2,1,0:T(4,128)(2,1)S(1)} async-done(((bf16[64,4,640]{2,1,0:T(4,128)(2,1)}), bf16[64,4,640]{2,1,0:T(4,128)(2,1)S(1)}, u32[]{:S(2)}, u32[]{:S(2)}) %all-to-all-start.3) | async-done | bytes 327712 | tf_op jit(solution)/shard_map/all_to_all | solution.py:106
  143.4 1.4 fusion.1
  (58 shorter events, 13.3 us)
Async XLA Ops:
  0.6 1.2 copy-start
  3.2 44.7 %all-to-all-start = ((bf16[64,4,512]{2,1,0:T(4,128)(2,1)}), bf16[64,4,512]{2,1,0:T(4,128)(2,1)S(1)}, u32[]{:S(2)}, u32[]{:S(2)}) async-start(bf16[64,4,512]{2,1,0:T(4,128)(2,1)} %copy.26), calls=%async_computation | async-start | bytes 524288 | tf_op jit(solution)/shard_map/all_to_all | solution.py:70
  48.1 5.3 %copy-start.1 = (bf16[192,4096]{1,0:T(8,128)(2,1)S(1)}, bf16[192,4096]{1,0:T(8,128)(2,1)}, u32[]{:S(2)}) copy-start(bf16[192,4096]{1,0:T(8,128)(2,1)} %param.11) | copy-start | bytes 4718596
  49.2 47.6 %all-to-all-start.1 = ((bf16[8,128,512]{2,1,0:T(8,128)(2,1)}), bf16[8,128,512]{2,1,0:T(8,128)(2,1)}, u32[]{:S(2)}, u32[]{:S(2)}) async-start(bf16[8,128,512]{2,1,0:T(8,128)(2,1)} %broadcast_in_dim.85), calls=%async_computation.1 | async-start | bytes 2097152 | tf_op jit(solution)/shard_map/all_to_all | solution.py:41
  53.4 4.8 %copy-start.2 = (bf16[4096,128]{1,0:T(8,128)(2,1)S(1)}, bf16[4096,128]{1,0:T(8,128)(2,1)}, u32[]{:S(2)}) copy-start(bf16[4096,128]{1,0:T(8,128)(2,1)} %param.7) | copy-start | bytes 3145732
  54.4 28.6 %collective-permute-start = (bf16[192,2048]{1,0:T(8,128)(2,1)}, bf16[192,2048]{1,0:T(8,128)(2,1)S(1)}, u32[]{:S(2)}, u32[]{:S(2)}) collective-permute-start(bf16[192,2048]{1,0:T(8,128)(2,1)} %constant_dynamic-slice_fusion), channel_id=1, source_target_pairs={{0,4},{4,0},{1,5},{5,1},{2,6},{6,2},{3,7},{7,3},{8,12},{12,8},{9,1... | collective-permute-start | bytes 2359304 | tf_op jit(solution)/shard_map/ppermute | solution.py:26
  83.9 21.4 %collective-permute-start.1 = (bf16[2,192,512]{2,1,0:T(8,128)(2,1)}, bf16[2,192,512]{2,1,0:T(8,128)(2,1)}, u32[]{:S(2)}, u32[]{:S(2)}) collective-permute-start(bf16[2,192,512]{2,1,0:T(8,128)(2,1)} %pad_maximum_fusion), channel_id=1, source_target_pairs={{0,1},{1,2},{2,3},{3,0},{4,5},{5,6},{6,7},{7,4},{8,9},{9,10},{10,1... | collective-permute-start | bytes 1179656 | tf_op jit(solution)/shard_map/ppermute | solution.py:33
  88.1 19.2 %collective-permute-start.2 = (bf16[2,192,512]{2,1,0:T(8,128)(2,1)}, bf16[2,192,512]{2,1,0:T(8,128)(2,1)}, u32[]{:S(2)}, u32[]{:S(2)}) collective-permute-start(bf16[2,192,512]{2,1,0:T(8,128)(2,1)} %pad_maximum_fusion.1), channel_id=1, source_target_pairs={{0,2},{1,3},{2,0},{3,1},{4,6},{5,7},{6,4},{7,5},{8,10},{9,11},{10,... | collective-permute-start | bytes 1179656 | tf_op jit(solution)/shard_map/ppermute | solution.py:33
  93.4 15.7 %collective-permute-start.3 = (bf16[2,192,512]{2,1,0:T(8,128)(2,1)}, bf16[2,192,512]{2,1,0:T(8,128)(2,1)}, u32[]{:S(2)}, u32[]{:S(2)}) collective-permute-start(bf16[2,192,512]{2,1,0:T(8,128)(2,1)} %pad_maximum_fusion.2), channel_id=1, source_target_pairs={{0,3},{1,0},{2,1},{3,2},{4,7},{5,4},{6,5},{7,6},{8,11},{9,8},{10,9... | collective-permute-start | bytes 1179656 | tf_op jit(solution)/shard_map/ppermute | solution.py:33
  96.8 2.4 %copy-start.3 = (bf16[4096,192]{0,1:T(8,128)(2,1)S(1)}, bf16[4096,192]{0,1:T(8,128)(2,1)}, u32[]{:S(2)}) copy-start(bf16[4096,192]{0,1:T(8,128)(2,1)} %param.10) | copy-start | bytes 4718596
  101.9 11.1 %all-to-all-start.2 = ((bf16[8,128,192]{1,2,0:T(8,128)(2,1)}), bf16[8,128,192]{1,2,0:T(8,128)(2,1)S(1)}, u32[]{:S(2)}, u32[]{:S(2)}) async-start(bf16[8,128,192]{1,2,0:T(8,128)(2,1)} %broadcast_in_dim.86), calls=%async_computation.2 | async-start | bytes 786432 | tf_op jit(solution)/shard_map/all_to_all | solution.py:41
  114.6 28.1 %all-to-all-start.3 = ((bf16[64,4,640]{2,1,0:T(4,128)(2,1)}), bf16[64,4,640]{2,1,0:T(4,128)(2,1)S(1)}, u32[]{:S(2)}, u32[]{:S(2)}) async-start(bf16[64,4,640]{2,1,0:T(4,128)(2,1)} %pad_maximum_fusion.3), calls=%async_computation.3 | async-start | bytes 655360 | tf_op jit(solution)/shard_map/all_to_all | solution.py:106

commit v2 on v1

--- a/solution.py
+++ b/solution.py
@@ -7,7 +7,8 @@
 
 DP = ("dp_0", "dp_1")
 EXPERT = ("ez", "zp", "x")
-SHARE = ("zp", "x")
+SHARE = ("x", "zp")
+TRADE = ("ez", "x", "zp")
 LANES = 128
 
 
@@ -19,22 +20,9 @@
     return jnp.stack([high, middle, low])
 
 
-def exchange_down(w_down, zp, x, n_zp, n_x, piece):
-    rows = w_down.shape[0]
-    half = n_x * piece
-    other = lax.dynamic_slice(w_down, (0, (1 - zp) * half), (rows, half))
-    other = lax.ppermute(other, "zp", [(i, 1 - i) for i in range(n_zp)])
-    down = jnp.zeros((n_zp, n_x, rows, piece), w_down.dtype)
-    for step in range(n_x):
-        block = (x + step) % n_x * piece
-        own_part = lax.dynamic_slice(w_down, (0, zp * half + block), (rows, piece))
-        part = jnp.stack([own_part, lax.dynamic_slice(other, (0, block), (rows, piece))])
-        if step:
-            part = lax.ppermute(part, "x", [(i, (i + step) % n_x) for i in range(n_x)])
-        source = (x + n_x - step) % n_x
-        down = lax.dynamic_update_slice(down, part[0][None, None], (zp, source, 0, 0))
-        down = lax.dynamic_update_slice(down, part[1][None, None], (1 - zp, source, 0, 0))
-    return down.reshape(n_zp * n_x, rows, piece)
+def add_partner(value, axis, bit):
+    size = lax.axis_size(axis)
+    return value + lax.ppermute(value, axis, [(i, i ^ bit) for i in range(size)])
 
 
 def copy_to(value, axes, count):
@@ -48,9 +36,7 @@
     rows_dev, width = token_rows.shape
     devices = lax.axis_size(EXPERT)
     n_dp = lax.axis_size(DP)
-    n_zp = lax.axis_size("zp")
-    n_x = lax.axis_size("x")
-    split = n_zp * n_x
+    split = lax.axis_size(SHARE)
     most = 2 * cap // devices
     piece = width // split
     hidden_cols = w_gate.shape[1]
@@ -67,13 +53,15 @@
     slot_rows = jnp.dot(pick_mat, token_rows, preferred_element_type=jnp.float32).astype(jnp.bfloat16)
     outgoing = slot_rows.reshape(experts, most, split, piece).transpose(0, 2, 1, 3).reshape(devices, most, piece)
     outgoing, logit_rows, member, taken = lax.optimization_barrier((outgoing, token_rows, member, taken))
-    arrived = lax.all_to_all(outgoing, EXPERT, 0, 0, tiled=True)
+    arrived = lax.all_to_all(outgoing, TRADE, 0, 0, tiled=True)
 
-    down = exchange_down(w_down, lax.axis_index("zp"), lax.axis_index("x"), n_zp, n_x, piece)
 
     mine = lax.dynamic_index_in_dim(picked, lax.axis_index("ez"), 0, keepdims=False)
     owner = mine // rows_dev
-    device_ids = jnp.arange(devices, dtype=jnp.int32)
+    places = jnp.arange(devices, dtype=jnp.int32)
+    n_zp = lax.axis_size("zp")
+    n_x = lax.axis_size("x")
+    device_ids = places // split * split + places % n_zp * n_x + places // n_zp % n_x
     first = jnp.sum((owner[None, :] < device_ids[:, None]).astype(jnp.int32), axis=1)
     count = jnp.sum((owner[None, :] == device_ids[:, None]).astype(jnp.int32), axis=1)
     slot_ids = jnp.arange(most, dtype=jnp.int32)[None, :]
@@ -87,8 +75,11 @@
     gate = jnp.einsum("kpd,kdf->pf", rows, w_gate.reshape(split, piece, hidden_cols), preferred_element_type=jnp.float32)
     upper = jnp.einsum("kpd,kdf->pf", rows, w_up.reshape(split, piece, hidden_cols), preferred_element_type=jnp.float32)
     hidden = (jax.nn.silu(gate) * upper).astype(jnp.bfloat16)
-    hidden = copy_to(hidden, SHARE, split)
-    expert_out = jnp.einsum("kpf,kfd->pd", hidden, down, preferred_element_type=jnp.float32).astype(jnp.bfloat16)
+    parts = jnp.einsum(
+        "pf,fkd->kpd", hidden, w_down.reshape(hidden_cols, split, piece), preferred_element_type=jnp.float32
+    ).astype(jnp.bfloat16)
+    parts = lax.all_to_all(parts, SHARE, 0, 0, tiled=True)
+    expert_out = jnp.sum(parts.astype(jnp.float32), axis=0).astype(jnp.bfloat16)
     spread = lax.dot_general(
         pack_mat, expert_out, (((0,), (0,)), ((), ())), preferred_element_type=jnp.float32
     ).astype(jnp.bfloat16)
@@ -98,12 +89,16 @@
     log_total = highest[:, 0] + jnp.log(jnp.sum(jnp.exp(logits - highest), axis=1))
     loss = jnp.sum(log_total * log_total)
     loss = lax.psum(loss, "dp_1")
-    loss = lax.psum(loss, "dp_0")
+    loss = jnp.broadcast_to(loss, (8, LANES))
+    loss = add_partner(loss, "dp_0", 1)
+    loss = add_partner(loss, "dp_0", 2)
+    loss = add_partner(loss, "dp_0", 4)
+    loss = loss[0, 0]
 
     terms = jnp.pad(three_terms(loss), (0, LANES - 3))
     terms = jnp.broadcast_to(terms[None, None, :], (devices, most, LANES))
     returned = jnp.concatenate([spread.reshape(devices, most, piece), terms], axis=2)
-    returned = lax.all_to_all(returned, EXPERT, 0, 0, tiled=True)
+    returned = lax.all_to_all(returned, TRADE, 0, 0, tiled=True)
     loss = jnp.sum(returned[:, 0, piece:].astype(jnp.float32))
     z_loss = loss / (n_dp * devices * rows_dev)
     full_out = (
@@ -119,9 +114,12 @@
     weights = jnp.where(taken, combine[:, None, :], 0.0).reshape(experts * most, rows_dev)
     coarse = weights.astype(jnp.bfloat16)
     fine = (weights - coarse.astype(jnp.float32)).astype(jnp.bfloat16)
-    over_slots = (((0,), (0,)), ((), ()))
-    mixed = lax.dot_general(coarse, full_out, over_slots, preferred_element_type=jnp.float32)
-    mixed = mixed + lax.dot_general(fine, full_out, over_slots, preferred_element_type=jnp.float32)
+    mixed = lax.dot_general(
+        jnp.concatenate([coarse, fine]),
+        jnp.concatenate([full_out, full_out]),
+        (((0,), (0,)), ((), ())),
+        preferred_element_type=jnp.float32,
+    )
     return (mixed.astype(jnp.bfloat16)[None], z_loss)
 
 

time: 148 us -> 140 us (0.946)
  the two profiles are of different devices: /device:TPU:8 before, /device:TPU:2 now
where the time goes in v2:
time: 140 us; the launch traced here: 139 us
  starting transfers between devices  50.5 us (36%)
  waiting for transfers between devices  47.5 us (34%)
  blocking collectives  20.6 us (15%)
  matrix products  7.75 us (6%)
  other arithmetic  5.83 us (4%)
  between operations  3.98 us (3%)
  local copies, waits for them, and re-layouts  2.82 us (2%)
    all_to_all x1, starting transfers between devices, layer(): arrived = lax.all_to_all(outgoing, TRADE, 0, 0, tiled=True)  22.3 us
    all_to_all x1, waiting for transfers between devices, layer(): returned = lax.all_to_all(returned, TRADE, 0, 0, tiled=True)  21.5 us
    all_to_all x1, waiting for transfers between devices, layer(): arrived = lax.all_to_all(outgoing, TRADE, 0, 0, tiled=True)  20.4 us
    all_to_all x1, blocking collectives, copy_to(): lax.all_to_all(jnp.broadcast_to(value[None], (count,) + value.shape), axe...  17.6 us
    ppermute x3, starting transfers between devices, add_partner(): lax.ppermute(value, axis, [(i, i ^ bit) for i in range(size)])  15.7 us
    all_to_all x1, starting transfers between devices, layer(): returned = lax.all_to_all(returned, TRADE, 0, 0, tiled=True)  7.02 us
    ppermute x3, waiting for transfers between devices, add_partner(): lax.ppermute(value, axis, [(i, i ^ bit) for i in range(size)])  5.56 us
    all_to_all x1, starting transfers between devices, layer(): parts = lax.all_to_all(parts, SHARE, 0, 0, tiled=True)  5.46 us
  transfers between devices with their start and end apart: 6, of which 5 were waited for; matrix products, arithmetic and copies ran while one was open for 4% of the time, Pallas kernels for 0%

profile of v2, /device:TPU:2, one launch (start us, length us, event | category | flops | bytes accessed | tf_op | source)
XLA Modules:
  0.0 139.0 jit_solution(6821671605006351766)
XLA Ops:
  0.7 0.8 subtract_bitcast_fusion
  2.3 0.9 copy.26
  3.2 22.3 %all-to-all-start = ((bf16[64,4,512]{2,1,0:T(4,128)(2,1)}), bf16[64,4,512]{2,1,0:T(4,128)(2,1)S(1)}, u32[]{:S(2)}, u32[]{:S(2)}) async-start(bf16[64,4,512]{2,1,0:T(4,128)(2,1)} %copy.26), calls=%async_computation | async-start | bytes 524288 | tf_op jit(solution)/shard_map/all_to_all | solution.py:56
  25.5 0.7 and_select_fusion.4
  26.6 20.4 %all-to-all-done = bf16[64,4,512]{2,1,0:T(4,128)(2,1)S(1)} async-done(((bf16[64,4,512]{2,1,0:T(4,128)(2,1)}), bf16[64,4,512]{2,1,0:T(4,128)(2,1)S(1)}, u32[]{:S(2)}, u32[]{:S(2)}) %all-to-all-start) | async-done | bytes 262176 | tf_op jit(solution)/shard_map/all_to_all | solution.py:56
  47.3 17.6 %all_to_all.20 = bf16[8,128,512]{2,1,0:T(8,128)(2,1)S(1)} all-to-all(bf16[8,128,512]{2,1,0:T(8,128)(2,1)S(1)} %broadcast_in_dim.79), channel_id=1, replica_groups=mesh['dp_0'=8,'dp_1'=2,'ez'=8,'zp'=2,'x'=4] {'x','zp'}, dimensions={0} | all-to-all | bytes 2097152 | tf_op jit(solution)/shard_map/all_to_all | solution.py:29
  65.5 4.4 %fusion.13 = bf16[8,128,512]{2,1,0:T(8,128)(2,1)} fusion(bf16[24,8,8,512]{3,2,1,0:T(8,128)(2,1)} %bitcast.102, bf16[8,128,512]{2,1,0:T(8,128)(2,1)S(1)} %all_to_all.20, bf16[24,8,8,512]{3,2,1,0:T(8,128)(2,1)} %bitcast.103, f32[128,192]{0,1:T(8,128)S(1)} %fusion.16), kind=kOutput, calls=%fused_computation.13 | convolution fusion | flops 403324928 | bytes 5341184 | tf_op jit(solution)/shard_map/pf,fkd->kpd/dot_general | solution.py:78
  69.9 5.5 %all-to-all-start.2 = ((bf16[8,128,512]{2,1,0:T(8,128)(2,1)}), bf16[8,128,512]{2,1,0:T(8,128)(2,1)S(1)}, u32[]{:S(2)}, u32[]{:S(2)}) async-start(bf16[8,128,512]{2,1,0:T(8,128)(2,1)} %fusion.13), calls=%async_computation.2 | async-start | bytes 2097152 | tf_op jit(solution)/shard_map/all_to_all | solution.py:81
  75.9 0.6 multiply_reduce_fusion
  76.5 3.1 %psum.7 = f32[]{:T(128)} all-reduce(f32[]{:T(128)} %multiply_reduce_fusion), channel_id=1, replica_groups=mesh['dp_0'=8,'dp_1'=2,'ez'=8,'zp'=2,'x'=4] {'dp_1'}, use_global_device_ids=true, to_apply=%region_10.11 | all-reduce | flops 1 | bytes 8 | tf_op jit(solution)/shard_map/psum | solution.py:91
  79.6 0.6 broadcast_in_dim.80
  80.2 3.5 %collective-permute-start = (f32[8,128]{1,0:T(8,128)S(1)}, f32[8,128]{1,0:T(8,128)S(1)}, u32[]{:S(2)}, u32[]{:S(2)}) collective-permute-start(f32[8,128]{1,0:T(8,128)S(1)} %broadcast_in_dim.80), channel_id=1, source_target_pairs={{0,128},{128,0},{256,384},{384,256},{512,640},{640,512},{768,896},... | collective-permute-start | bytes 12296 | tf_op jit(solution)/shard_map/ppermute | solution.py:25
  83.7 2.0 %collective-permute-done = f32[8,128]{1,0:T(8,128)S(1)} collective-permute-done((f32[8,128]{1,0:T(8,128)S(1)}, f32[8,128]{1,0:T(8,128)S(1)}, u32[]{:S(2)}, u32[]{:S(2)}) %collective-permute-start) | collective-permute-done | bytes 4128 | tf_op jit(solution)/shard_map/ppermute | solution.py:25
  85.7 0.6 broadcast_add_fusion
  86.4 4.5 %collective-permute-start.1 = (f32[8,128]{1,0:T(8,128)S(1)}, f32[8,128]{1,0:T(8,128)S(1)}, u32[]{:S(2)}, u32[]{:S(2)}) collective-permute-start(f32[8,128]{1,0:T(8,128)S(1)} %broadcast_add_fusion), channel_id=1, source_target_pairs={{0,256},{128,384},{256,0},{384,128},{512,768},{640,896},{768,512},... | collective-permute-start | bytes 12296 | tf_op jit(solution)/shard_map/ppermute | solution.py:25
  90.9 1.9 %collective-permute-done.1 = f32[8,128]{1,0:T(8,128)S(1)} collective-permute-done((f32[8,128]{1,0:T(8,128)S(1)}, f32[8,128]{1,0:T(8,128)S(1)}, u32[]{:S(2)}, u32[]{:S(2)}) %collective-permute-start.1) | collective-permute-done | bytes 4128 | tf_op jit(solution)/shard_map/ppermute | solution.py:25
  92.8 0.6 fusion.70
  93.5 7.7 %collective-permute-start.2 = (f32[8,128]{1,0:T(8,128)S(1)}, f32[8,128]{1,0:T(8,128)S(1)}, u32[]{:S(2)}, u32[]{:S(2)}) collective-permute-start(f32[8,128]{1,0:T(8,128)S(1)} %fusion.70), channel_id=1, source_target_pairs={{0,512},{128,640},{256,768},{384,896},{512,0},{640,128},{768,256},... | collective-permute-start | bytes 12296 | tf_op jit(solution)/shard_map/ppermute | solution.py:25
  101.2 1.7 %collective-permute-done.2 = f32[8,128]{1,0:T(8,128)S(1)} collective-permute-done((f32[8,128]{1,0:T(8,128)S(1)}, f32[8,128]{1,0:T(8,128)S(1)}, u32[]{:S(2)}, u32[]{:S(2)}) %collective-permute-start.2) | collective-permute-done | bytes 4128 | tf_op jit(solution)/shard_map/ppermute | solution.py:25
  105.3 0.9 pad_maximum_fusion
  106.2 7.0 %all-to-all-start.3 = ((bf16[64,4,640]{2,1,0:T(4,128)(2,1)}), bf16[64,4,640]{2,1,0:T(4,128)(2,1)S(1)}, u32[]{:S(2)}, u32[]{:S(2)}) async-start(bf16[64,4,640]{2,1,0:T(4,128)(2,1)} %pad_maximum_fusion), calls=%async_computation.3 | async-start | bytes 655360 | tf_op jit(solution)/shard_map/all_to_all | solution.py:101
  113.3 21.5 %all-to-all-done.3 = bf16[64,4,640]{2,1,0:T(4,128)(2,1)S(1)} async-done(((bf16[64,4,640]{2,1,0:T(4,128)(2,1)}), bf16[64,4,640]{2,1,0:T(4,128)(2,1)S(1)}, u32[]{:S(2)}, u32[]{:S(2)}) %all-to-all-start.3) | async-done | bytes 327712 | tf_op jit(solution)/shard_map/all_to_all | solution.py:101
  135.1 0.7 fusion.46
  136.4 1.4 %fusion = bf16[1,128,4096]{2,1,0:T(8,128)(2,1)} fusion(bf16[32,4096]{1,0:T(8,128)(2,1)S(1)} %bitcast.109, bf16[32,128]{1,0:T(8,128)(2,1)S(1)} %get-tuple-element.12, bf16[32,128]{1,0:T(8,128)(2,1)S(1)} %get-tuple-element.13), kind=kOutput, calls=%fused_computation.1 | convolution fusion | flops 68714496 | bytes 1327104 | tf_op jit(solution)/shard_map/dot_general | solution.py:117
  (42 shorter events, 4.1 us)
Async XLA Ops:
  0.6 1.2 copy-start
  3.2 43.8 %all-to-all-start = ((bf16[64,4,512]{2,1,0:T(4,128)(2,1)}), bf16[64,4,512]{2,1,0:T(4,128)(2,1)S(1)}, u32[]{:S(2)}, u32[]{:S(2)}) async-start(bf16[64,4,512]{2,1,0:T(4,128)(2,1)} %copy.26), calls=%async_computation | async-start | bytes 524288 | tf_op jit(solution)/shard_map/all_to_all | solution.py:56
  47.2 17.7 %copy-start.2 = (bf16[4096,192]{0,1:T(8,128)(2,1)S(1)}, bf16[4096,192]{0,1:T(8,128)(2,1)}, u32[]{:S(2)}) copy-start(bf16[4096,192]{0,1:T(8,128)(2,1)} %param.9) | copy-start | bytes 4718596
  69.9 5.5 %copy-start.1 = (bf16[4096,128]{1,0:T(8,128)(2,1)S(1)}, bf16[4096,128]{1,0:T(8,128)(2,1)}, u32[]{:S(2)}) copy-start(bf16[4096,128]{1,0:T(8,128)(2,1)} %param.7) | copy-start | bytes 3145732
  69.9 34.9 %all-to-all-start.2 = ((bf16[8,128,512]{2,1,0:T(8,128)(2,1)}), bf16[8,128,512]{2,1,0:T(8,128)(2,1)S(1)}, u32[]{:S(2)}, u32[]{:S(2)}) async-start(bf16[8,128,512]{2,1,0:T(8,128)(2,1)} %fusion.13), calls=%async_computation.2 | async-start | bytes 2097152 | tf_op jit(solution)/shard_map/all_to_all | solution.py:81
  80.2 5.5 %collective-permute-start = (f32[8,128]{1,0:T(8,128)S(1)}, f32[8,128]{1,0:T(8,128)S(1)}, u32[]{:S(2)}, u32[]{:S(2)}) collective-permute-start(f32[8,128]{1,0:T(8,128)S(1)} %broadcast_in_dim.80), channel_id=1, source_target_pairs={{0,128},{128,0},{256,384},{384,256},{512,640},{640,512},{768,896},... | collective-permute-start | bytes 12296 | tf_op jit(solution)/shard_map/ppermute | solution.py:25
  86.4 6.4 %collective-permute-start.1 = (f32[8,128]{1,0:T(8,128)S(1)}, f32[8,128]{1,0:T(8,128)S(1)}, u32[]{:S(2)}, u32[]{:S(2)}) collective-permute-start(f32[8,128]{1,0:T(8,128)S(1)} %broadcast_add_fusion), channel_id=1, source_target_pairs={{0,256},{128,384},{256,0},{384,128},{512,768},{640,896},{768,512},... | collective-permute-start | bytes 12296 | tf_op jit(solution)/shard_map/ppermute | solution.py:25
  93.5 9.4 %collective-permute-start.2 = (f32[8,128]{1,0:T(8,128)S(1)}, f32[8,128]{1,0:T(8,128)S(1)}, u32[]{:S(2)}, u32[]{:S(2)}) collective-permute-start(f32[8,128]{1,0:T(8,128)S(1)} %fusion.70), channel_id=1, source_target_pairs={{0,512},{128,640},{256,768},{384,896},{512,0},{640,128},{768,256},... | collective-permute-start | bytes 12296 | tf_op jit(solution)/shard_map/ppermute | solution.py:25
  106.2 28.7 %all-to-all-start.3 = ((bf16[64,4,640]{2,1,0:T(4,128)(2,1)}), bf16[64,4,640]{2,1,0:T(4,128)(2,1)S(1)}, u32[]{:S(2)}, u32[]{:S(2)}) async-start(bf16[64,4,640]{2,1,0:T(4,128)(2,1)} %pad_maximum_fusion), calls=%async_computation.3 | async-start | bytes 655360 | tf_op jit(solution)/shard_map/all_to_all | solution.py:101

commit v3 on v2

--- a/solution.py
+++ b/solution.py
@@ -23,6 +23,29 @@
 def add_partner(value, axis, bit):
     size = lax.axis_size(axis)
     return value + lax.ppermute(value, axis, [(i, i ^ bit) for i in range(size)])
+
+
+def exchange_down(w_down, later, core, zp, x, n_core, n_zp, n_x):
+    rows, width = w_down.shape
+    piece = width // (n_x * n_zp)
+    half = piece // n_core
+
+    def columns(weight, column, row):
+        return lax.dynamic_slice(weight, (0, (column * n_zp + row) * piece + core * half), (rows, half))
+
+    other = jnp.concatenate([columns(w_down, column, 1 - zp) for column in range(n_x)], axis=1)
+    other = lax.ppermute(other, "zp", [(i, 1 - i) for i in range(n_zp)])
+    mine = jnp.zeros((n_x * n_zp, rows, half), w_down.dtype)
+    for step in range(n_x):
+        target = (x + step) % n_x
+        own_part = columns(later, target, zp)
+        other_part = lax.dynamic_slice(other, (0, target * half), (rows, half))
+        part = jnp.stack([jnp.where(zp == 0, own_part, other_part), jnp.where(zp == 0, other_part, own_part)])
+        if step:
+            part = lax.ppermute(part, "x", [(i, (i + step) % n_x) for i in range(n_x)])
+        mine = lax.dynamic_update_slice(mine, part, ((x + n_x - step) % n_x * n_zp, 0, 0))
+    theirs = lax.ppermute(mine, "dp_1", [(i, 1 - i) for i in range(n_core)])
+    return mine, theirs
 
 
 def copy_to(value, axes, count):
@@ -51,16 +74,22 @@
     taken = member[:, None, :] & (rank[:, None, :] == slots[None, :, None])
     pick_mat = taken.reshape(experts * most, rows_dev).astype(jnp.bfloat16)
     slot_rows = jnp.dot(pick_mat, token_rows, preferred_element_type=jnp.float32).astype(jnp.bfloat16)
+    logits = jnp.dot(token_rows, router_weight, preferred_element_type=jnp.float32)
+    highest = jnp.max(logits, axis=1, keepdims=True)
+    log_total = highest[:, 0] + jnp.log(jnp.sum(jnp.exp(logits - highest), axis=1))
+
+    terms = jnp.pad(three_terms(log_total * log_total), ((0, most - 3), (0, 0)))
     outgoing = slot_rows.reshape(experts, most, split, piece).transpose(0, 2, 1, 3).reshape(devices, most, piece)
-    outgoing, logit_rows, member, taken = lax.optimization_barrier((outgoing, token_rows, member, taken))
+    outgoing = jnp.concatenate([outgoing, jnp.broadcast_to(terms[None], (devices, most, rows_dev))], axis=2)
+    outgoing, logits, member, taken, later = lax.optimization_barrier((outgoing, logits, member, taken, w_down))
     arrived = lax.all_to_all(outgoing, TRADE, 0, 0, tiled=True)
-
+    core, zp, x = (lax.axis_index(name) for name in ("dp_1", "zp", "x"))
+    n_core, n_zp, n_x = (lax.axis_size(name) for name in ("dp_1", "zp", "x"))
+    down_mine, down_theirs = exchange_down(w_down, later, core, zp, x, n_core, n_zp, n_x)
 
     mine = lax.dynamic_index_in_dim(picked, lax.axis_index("ez"), 0, keepdims=False)
     owner = mine // rows_dev
     places = jnp.arange(devices, dtype=jnp.int32)
-    n_zp = lax.axis_size("zp")
-    n_x = lax.axis_size("x")
     device_ids = places // split * split + places % n_zp * n_x + places // n_zp % n_x
     first = jnp.sum((owner[None, :] < device_ids[:, None]).astype(jnp.int32), axis=1)
     count = jnp.sum((owner[None, :] == device_ids[:, None]).astype(jnp.int32), axis=1)
@@ -68,42 +97,33 @@
     target = jnp.where(slot_ids < count[:, None], first[:, None] + slot_ids, -1).reshape(-1)
     pack_mat = (jnp.arange(cap, dtype=jnp.int32)[:, None] == target[None, :]).astype(jnp.bfloat16)
     packed = jnp.dot(
-        pack_mat, arrived.reshape(devices * most, piece), preferred_element_type=jnp.float32
+        pack_mat, arrived[:, :, :piece].reshape(devices * most, piece), preferred_element_type=jnp.float32
     ).astype(jnp.bfloat16)
 
     rows = copy_to(packed, SHARE, split)
     gate = jnp.einsum("kpd,kdf->pf", rows, w_gate.reshape(split, piece, hidden_cols), preferred_element_type=jnp.float32)
     upper = jnp.einsum("kpd,kdf->pf", rows, w_up.reshape(split, piece, hidden_cols), preferred_element_type=jnp.float32)
     hidden = (jax.nn.silu(gate) * upper).astype(jnp.bfloat16)
-    parts = jnp.einsum(
-        "pf,fkd->kpd", hidden, w_down.reshape(hidden_cols, split, piece), preferred_element_type=jnp.float32
-    ).astype(jnp.bfloat16)
-    parts = lax.all_to_all(parts, SHARE, 0, 0, tiled=True)
-    expert_out = jnp.sum(parts.astype(jnp.float32), axis=0).astype(jnp.bfloat16)
+    hidden = copy_to(hidden, SHARE, split)
+    out_mine = jnp.einsum("kpf,kfd->pd", hidden, down_mine, preferred_element_type=jnp.float32).astype(jnp.bfloat16)
+    out_theirs = jnp.einsum("kpf,kfd->pd", hidden, down_theirs, preferred_element_type=jnp.float32).astype(jnp.bfloat16)
+    low = jnp.where(core == 0, out_mine, out_theirs)
+    high = jnp.where(core == 0, out_theirs, out_mine)
+    expert_out = jnp.concatenate([low, high], axis=1)
     spread = lax.dot_general(
         pack_mat, expert_out, (((0,), (0,)), ((), ())), preferred_element_type=jnp.float32
     ).astype(jnp.bfloat16)
 
-    logits = jnp.dot(logit_rows, router_weight, preferred_element_type=jnp.float32)
-    highest = jnp.max(logits, axis=1, keepdims=True)
-    log_total = highest[:, 0] + jnp.log(jnp.sum(jnp.exp(logits - highest), axis=1))
-    loss = jnp.sum(log_total * log_total)
+    returned = lax.all_to_all(spread.reshape(devices, most, piece), TRADE, 0, 0, tiled=True)
+    full_out = returned.reshape(experts, split, most, piece).transpose(0, 2, 1, 3).reshape(experts * most, width)
+
+    loss = jnp.sum(arrived[:, :, piece:].astype(jnp.float32))
     loss = lax.psum(loss, "dp_1")
     loss = jnp.broadcast_to(loss, (8, LANES))
     loss = add_partner(loss, "dp_0", 1)
     loss = add_partner(loss, "dp_0", 2)
     loss = add_partner(loss, "dp_0", 4)
-    loss = loss[0, 0]
-
-    terms = jnp.pad(three_terms(loss), (0, LANES - 3))
-    terms = jnp.broadcast_to(terms[None, None, :], (devices, most, LANES))
-    returned = jnp.concatenate([spread.reshape(devices, most, piece), terms], axis=2)
-    returned = lax.all_to_all(returned, TRADE, 0, 0, tiled=True)
-    loss = jnp.sum(returned[:, 0, piece:].astype(jnp.float32))
-    z_loss = loss / (n_dp * devices * rows_dev)
-    full_out = (
-        returned[:, :, :piece].reshape(experts, split, most, piece).transpose(0, 2, 1, 3).reshape(experts * most, width)
-    )
+    z_loss = loss[0, 0] / (n_dp * devices * rows_dev)
 
     window = logits[:, :experts].T
     peak = jnp.max(jnp.where(member, window, -1e30), axis=0, keepdims=True)

time: 140 us -> 149 us (1.064)
  the two profiles are of different devices: /device:TPU:2 before, /device:TPU:16 now
where the time goes in v3:
time: 149 us
  starting transfers between devices  67.7 us (45%)
  waiting for transfers between devices  54 us (36%)
  local copies, waits for them, and re-layouts  8.62 us (6%)
  matrix products  7.34 us (5%)
  other arithmetic  4.71 us (3%)
  blocking collectives  3.24 us (2%)
  between operations  3 us (2%)
    all_to_all x1, waiting for transfers between devices, layer(): arrived = lax.all_to_all(outgoing, TRADE, 0, 0, tiled=True)  24 us
    all_to_all x1, starting transfers between devices, layer(): arrived = lax.all_to_all(outgoing, TRADE, 0, 0, tiled=True)  22.2 us
    ppermute x1, waiting for transfers between devices, exchange_down(): other = lax.ppermute(other, 'zp', [(i, 1 - i) for i in range(n_zp)])  15.7 us
    ppermute x3, starting transfers between devices, exchange_down(): part = lax.ppermute(part, 'x', [(i, (i + step) % n_x) for i in range(n_x)])  13 us
    ppermute x3, starting transfers between devices, add_partner(): lax.ppermute(value, axis, [(i, i ^ bit) for i in range(size)])  10.8 us
    ppermute x3, waiting for transfers between devices, add_partner(): lax.ppermute(value, axis, [(i, i ^ bit) for i in range(size)])  8.49 us
    all_to_all x2, starting transfers between devices, copy_to(): lax.all_to_all(jnp.broadcast_to(value[None], (count,) + value.shape), axe...  8.05 us
    all_to_all x1, starting transfers between devices, layer(): lax.all_to_all(spread.reshape(devices, most, piece), TRADE, 0, 0, tiled=T...  7.78 us
  transfers between devices with their start and end apart: 12, of which 6 were waited for; matrix products, arithmetic and copies ran while one was open for 9% of the time, Pallas kernels for 0%

profile of v3, /device:TPU:16, one launch (start us, length us, event | category | flops | bytes accessed | tf_op | source)
XLA Modules:
  0.0 148.6 jit_solution(8088197592345457295)
XLA Ops:
  0.7 1.2 copy-done
  1.9 1.8 %fusion.58 = (f32[128]{0:T(128)S(1)}, f32[128,128]{0,1:T(8,128)S(1)}) fusion(bf16[4096,128]{1,0:T(8,128)(2,1)} %param.7, bf16[1,128,4096]{2,1,0:T(8,128)(2,1)S(1)} %copy-done), kind=kOutput, calls=%fused_computation.120 | convolution fusion | flops 134233984 | bytes 2163200 | tf_op jit(solution)/shard_map/dot_general | solution.py:77
  5.5 22.2 %all-to-all-start = ((bf16[64,4,640]{2,1,0:T(4,128)(2,1)}), bf16[64,4,640]{2,1,0:T(4,128)(2,1)S(1)}, u32[]{:S(2)}, u32[]{:S(2)}) async-start(bf16[64,4,640]{2,1,0:T(4,128)(2,1)} %copy.26), calls=%async_computation | async-start | bytes 655360 | tf_op jit(solution)/shard_map/all_to_all | solution.py:85
  28.2 24.0 %all-to-all-done = bf16[64,4,640]{2,1,0:T(4,128)(2,1)S(1)} async-done(((bf16[64,4,640]{2,1,0:T(4,128)(2,1)}), bf16[64,4,640]{2,1,0:T(4,128)(2,1)S(1)}, u32[]{:S(2)}, u32[]{:S(2)}) %all-to-all-start) | async-done | bytes 327712 | tf_op jit(solution)/shard_map/all_to_all | solution.py:85
  53.6 4.6 %all-to-all-start.1 = ((bf16[8,128,512]{2,1,0:T(8,128)(2,1)}), bf16[8,128,512]{2,1,0:T(8,128)(2,1)S(1)}, u32[]{:S(2)}, u32[]{:S(2)}) async-start(bf16[8,128,512]{2,1,0:T(8,128)(2,1)} %broadcast_in_dim.89), calls=%async_computation.1 | async-start | bytes 2097152 | tf_op jit(solution)/shard_map/all_to_all | solution.py:52
  59.3 3.9 %collective-permute-start = (bf16[192,1024]{1,0:T(8,128)(2,1)S(1)}, bf16[192,1024]{1,0:T(8,128)(2,1)S(1)}, u32[]{:S(2)}, u32[]{:S(2)}) collective-permute-start(bf16[192,1024]{1,0:T(8,128)(2,1)S(1)} %pad_maximum_fusion), channel_id=1, source_target_pairs={{0,4},{4,0},{1,5},{5,1},{2,6},{6,2},{3,7},{7,3},{8,12},{12,8},{9,1... | collective-permute-start | bytes 1179656 | tf_op jit(solution)/shard_map/ppermute | solution.py:37
  63.4 15.7 %collective-permute-done = bf16[192,1024]{1,0:T(8,128)(2,1)S(1)} collective-permute-done((bf16[192,1024]{1,0:T(8,128)(2,1)S(1)}, bf16[192,1024]{1,0:T(8,128)(2,1)S(1)}, u32[]{:S(2)}, u32[]{:S(2)}) %collective-permute-start) | collective-permute-done | bytes 393248 | tf_op jit(solution)/shard_map/ppermute | solution.py:37
  79.0 1.2 select_bitcast_fusion.1
  80.9 3.4 %collective-permute-start.1 = (bf16[2,192,256]{2,1,0:T(8,128)(2,1)}, bf16[2,192,256]{2,1,0:T(8,128)(2,1)}, u32[]{:S(2)}, u32[]{:S(2)}) collective-permute-start(bf16[2,192,256]{2,1,0:T(8,128)(2,1)} %pad_maximum_fusion.2), channel_id=1, source_target_pairs={{0,1},{1,2},{2,3},{3,0},{4,5},{5,6},{6,7},{7,4},{8,9},{9,10},{10,1... | collective-permute-start | bytes 589832 | tf_op jit(solution)/shard_map/ppermute | solution.py:45
  84.4 4.5 %collective-permute-start.2 = (bf16[2,192,256]{2,1,0:T(8,128)(2,1)S(1)}, bf16[2,192,256]{2,1,0:T(8,128)(2,1)S(1)}, u32[]{:S(2)}, u32[]{:S(2)}) collective-permute-start(bf16[2,192,256]{2,1,0:T(8,128)(2,1)S(1)} %pad_maximum_fusion.3), channel_id=1, source_target_pairs={{0,2},{1,3},{2,0},{3,1},{4,6},{5,7},{6,4},{7,5},{8,10},{9,11},{10,... | collective-permute-start | bytes 589832 | tf_op jit(solution)/shard_map/ppermute | solution.py:45
  88.9 2.1 %fusion.9 = f32[128,192]{0,1:T(8,128)S(1)} fusion(bf16[8,128,512]{2,1,0:T(8,128)(2,1)S(1)} %all-to-all-done.1, bf16[24,8,8,512]{3,2,1,0:T(8,128)(2,1)} %bitcast.128), kind=kOutput, calls=%fused_computation.15 | convolution fusion | flops 201326592 | bytes 2719744 | tf_op jit(solution)/shard_map/kpd,kdf->pf/dot_general | solution.py:104
  92.4 3.5 %all-to-all-start.2 = ((bf16[8,128,192]{1,2,0:T(8,128)(2,1)}), bf16[8,128,192]{1,2,0:T(8,128)(2,1)S(1)}, u32[]{:S(2)}, u32[]{:S(2)}) async-start(bf16[8,128,192]{1,2,0:T(8,128)(2,1)} %broadcast_in_dim.90), calls=%async_computation.2 | async-start | bytes 786432 | tf_op jit(solution)/shard_map/all_to_all | solution.py:52
  95.9 5.1 %collective-permute-start.3 = (bf16[2,192,256]{2,1,0:T(8,128)(2,1)S(1)}, bf16[2,192,256]{2,1,0:T(8,128)(2,1)S(1)}, u32[]{:S(2)}, u32[]{:S(2)}) collective-permute-start(bf16[2,192,256]{2,1,0:T(8,128)(2,1)S(1)} %pad_maximum_fusion.4), channel_id=1, source_target_pairs={{0,3},{1,0},{2,1},{3,2},{4,7},{5,4},{6,5},{7,6},{8,11},{9,8},{10,9... | collective-permute-start | bytes 589832 | tf_op jit(solution)/shard_map/ppermute | solution.py:45
  102.1 2.3 %collective-permute-done.3 = bf16[2,192,256]{2,1,0:T(8,128)(2,1)S(1)} collective-permute-done((bf16[2,192,256]{2,1,0:T(8,128)(2,1)S(1)}, bf16[2,192,256]{2,1,0:T(8,128)(2,1)S(1)}, u32[]{:S(2)}, u32[]{:S(2)}) %collective-permute-start.3) | collective-permute-done | bytes 196640 | tf_op jit(solution)/shard_map/ppermute | solution.py:45
  104.4 1.9 %collective-permute-start.4 = (bf16[8,192,256]{2,1,0:T(8,128)(2,1)S(1)}, bf16[8,192,256]{2,1,0:T(8,128)(2,1)S(1)}, u32[]{:S(2)}, u32[]{:S(2)}) collective-permute-start(bf16[8,192,256]{2,1,0:T(8,128)(2,1)S(1)} %constant_dynamic-update-slice_fusion), channel_id=1, source_target_pairs={{0,64},{64,0},{1,65},{65,1},{2,66},{66,2},{3,67},{67,3},{4,68},{68... | collective-permute-start | bytes 2359304 | tf_op jit(solution)/shard_map/ppermute | solution.py:47
  107.0 3.2 %psum.7 = f32[]{:T(128)} all-reduce(f32[]{:T(128)} %convert_reduce_fusion), channel_id=1, replica_groups=mesh['dp_0'=8,'dp_1'=2,'ez'=8,'zp'=2,'x'=4] {'dp_1'}, use_global_device_ids=true, to_apply=%region_9.10 | all-reduce | flops 1 | bytes 8 | tf_op jit(solution)/shard_map/psum | solution.py:121
  110.9 3.5 %collective-permute-start.5 = (f32[8,128]{1,0:T(8,128)S(1)}, f32[8,128]{1,0:T(8,128)S(1)}, u32[]{:S(2)}, u32[]{:S(2)}) collective-permute-start(f32[8,128]{1,0:T(8,128)S(1)} %broadcast_in_dim.93), channel_id=1, source_target_pairs={{0,128},{128,0},{256,384},{384,256},{512,640},{640,512},{768,896},... | collective-permute-start | bytes 12296 | tf_op jit(solution)/shard_map/ppermute | solution.py:25
  116.2 7.8 %all-to-all-start.3 = ((bf16[64,4,512]{2,1,0:T(4,128)(2,1)}), bf16[64,4,512]{2,1,0:T(4,128)(2,1)S(1)}, u32[]{:S(2)}, u32[]{:S(2)}) async-start(bf16[64,4,512]{2,1,0:T(4,128)(2,1)} %reshape.265), calls=%async_computation.3 | async-start | bytes 524288 | tf_op jit(solution)/shard_map/all_to_all | solution.py:117
  124.6 2.2 %collective-permute-start.6 = (f32[8,128]{1,0:T(8,128)S(1)}, f32[8,128]{1,0:T(8,128)S(1)}, u32[]{:S(2)}, u32[]{:S(2)}) collective-permute-start(f32[8,128]{1,0:T(8,128)S(1)} %broadcast_add_fusion), channel_id=1, source_target_pairs={{0,256},{128,384},{256,0},{384,128},{512,768},{640,896},{768,512},... | collective-permute-start | bytes 12296 | tf_op jit(solution)/shard_map/ppermute | solution.py:25
  126.9 4.1 %collective-permute-done.6 = f32[8,128]{1,0:T(8,128)S(1)} collective-permute-done((f32[8,128]{1,0:T(8,128)S(1)}, f32[8,128]{1,0:T(8,128)S(1)}, u32[]{:S(2)}, u32[]{:S(2)}) %collective-permute-start.6) | collective-permute-done | bytes 4128 | tf_op jit(solution)/shard_map/ppermute | solution.py:25
  131.7 5.0 %collective-permute-start.7 = (f32[8,128]{1,0:T(8,128)S(1)}, f32[8,128]{1,0:T(8,128)S(1)}, u32[]{:S(2)}, u32[]{:S(2)}) collective-permute-start(f32[8,128]{1,0:T(8,128)S(1)} %fusion.69), channel_id=1, source_target_pairs={{0,512},{128,640},{256,768},{384,896},{512,0},{640,128},{768,256},... | collective-permute-start | bytes 12296 | tf_op jit(solution)/shard_map/ppermute | solution.py:25
  136.7 4.4 %collective-permute-done.7 = f32[8,128]{1,0:T(8,128)S(1)} collective-permute-done((f32[8,128]{1,0:T(8,128)S(1)}, f32[8,128]{1,0:T(8,128)S(1)}, u32[]{:S(2)}, u32[]{:S(2)}) %collective-permute-start.7) | collective-permute-done | bytes 4128 | tf_op jit(solution)/shard_map/ppermute | solution.py:25
  142.3 3.6 %all-to-all-done.3 = bf16[64,4,512]{2,1,0:T(4,128)(2,1)S(1)} async-done(((bf16[64,4,512]{2,1,0:T(4,128)(2,1)}), bf16[64,4,512]{2,1,0:T(4,128)(2,1)S(1)}, u32[]{:S(2)}, u32[]{:S(2)}) %all-to-all-start.3) | async-done | bytes 262176 | tf_op jit(solution)/shard_map/all_to_all | solution.py:117
  146.0 1.4 fusion
  (67 shorter events, 13.0 us)
Async XLA Ops:
  0.6 1.2 copy-start
  0.6 3.1 %copy-start.1 = (s32[1,8,128]{2,1,0:T(8,128)S(1)}, s32[1,8,128]{2,1,0:T(8,128)}, u32[]{:S(2)}) copy-start(s32[1,8,128]{2,1,0:T(8,128)} %param.8) | copy-start | bytes 12292
  5.5 46.6 %all-to-all-start = ((bf16[64,4,640]{2,1,0:T(4,128)(2,1)}), bf16[64,4,640]{2,1,0:T(4,128)(2,1)S(1)}, u32[]{:S(2)}, u32[]{:S(2)}) async-start(bf16[64,4,640]{2,1,0:T(4,128)(2,1)} %copy.26), calls=%async_computation | async-start | bytes 655360 | tf_op jit(solution)/shard_map/all_to_all | solution.py:85
  53.6 35.3 %all-to-all-start.1 = ((bf16[8,128,512]{2,1,0:T(8,128)(2,1)}), bf16[8,128,512]{2,1,0:T(8,128)(2,1)S(1)}, u32[]{:S(2)}, u32[]{:S(2)}) async-start(bf16[8,128,512]{2,1,0:T(8,128)(2,1)} %broadcast_in_dim.89), calls=%async_computation.1 | async-start | bytes 2097152 | tf_op jit(solution)/shard_map/all_to_all | solution.py:52
  59.3 19.7 %collective-permute-start = (bf16[192,1024]{1,0:T(8,128)(2,1)S(1)}, bf16[192,1024]{1,0:T(8,128)(2,1)S(1)}, u32[]{:S(2)}, u32[]{:S(2)}) collective-permute-start(bf16[192,1024]{1,0:T(8,128)(2,1)S(1)} %pad_maximum_fusion), channel_id=1, source_target_pairs={{0,4},{4,0},{1,5},{5,1},{2,6},{6,2},{3,7},{7,3},{8,12},{12,8},{9,1... | collective-permute-start | bytes 1179656 | tf_op jit(solution)/shard_map/ppermute | solution.py:37
  80.9 20.2 %collective-permute-start.1 = (bf16[2,192,256]{2,1,0:T(8,128)(2,1)}, bf16[2,192,256]{2,1,0:T(8,128)(2,1)}, u32[]{:S(2)}, u32[]{:S(2)}) collective-permute-start(bf16[2,192,256]{2,1,0:T(8,128)(2,1)} %pad_maximum_fusion.2), channel_id=1, source_target_pairs={{0,1},{1,2},{2,3},{3,0},{4,5},{5,6},{6,7},{7,4},{8,9},{9,10},{10,1... | collective-permute-start | bytes 589832 | tf_op jit(solution)/shard_map/ppermute | solution.py:45
  84.4 17.7 %collective-permute-start.2 = (bf16[2,192,256]{2,1,0:T(8,128)(2,1)S(1)}, bf16[2,192,256]{2,1,0:T(8,128)(2,1)S(1)}, u32[]{:S(2)}, u32[]{:S(2)}) collective-permute-start(bf16[2,192,256]{2,1,0:T(8,128)(2,1)S(1)} %pad_maximum_fusion.3), channel_id=1, source_target_pairs={{0,2},{1,3},{2,0},{3,1},{4,6},{5,7},{6,4},{7,5},{8,10},{9,11},{10,... | collective-permute-start | bytes 589832 | tf_op jit(solution)/shard_map/ppermute | solution.py:45
  88.9 2.1 %copy-start.2 = (bf16[4096,192]{0,1:T(8,128)(2,1)S(1)}, bf16[4096,192]{0,1:T(8,128)(2,1)}, u32[]{:S(2)}) copy-start(bf16[4096,192]{0,1:T(8,128)(2,1)} %param.10) | copy-start | bytes 4718596
  92.4 22.0 %all-to-all-start.2 = ((bf16[8,128,192]{1,2,0:T(8,128)(2,1)}), bf16[8,128,192]{1,2,0:T(8,128)(2,1)S(1)}, u32[]{:S(2)}, u32[]{:S(2)}) async-start(bf16[8,128,192]{1,2,0:T(8,128)(2,1)} %broadcast_in_dim.90), calls=%async_computation.2 | async-start | bytes 786432 | tf_op jit(solution)/shard_map/all_to_all | solution.py:52
  95.9 8.4 %collective-permute-start.3 = (bf16[2,192,256]{2,1,0:T(8,128)(2,1)S(1)}, bf16[2,192,256]{2,1,0:T(8,128)(2,1)S(1)}, u32[]{:S(2)}, u32[]{:S(2)}) collective-permute-start(bf16[2,192,256]{2,1,0:T(8,128)(2,1)S(1)} %pad_maximum_fusion.4), channel_id=1, source_target_pairs={{0,3},{1,0},{2,1},{3,2},{4,7},{5,4},{6,5},{7,6},{8,11},{9,8},{10,9... | collective-permute-start | bytes 589832 | tf_op jit(solution)/shard_map/ppermute | solution.py:45
  104.4 10.0 %collective-permute-start.4 = (bf16[8,192,256]{2,1,0:T(8,128)(2,1)S(1)}, bf16[8,192,256]{2,1,0:T(8,128)(2,1)S(1)}, u32[]{:S(2)}, u32[]{:S(2)}) collective-permute-start(bf16[8,192,256]{2,1,0:T(8,128)(2,1)S(1)} %constant_dynamic-update-slice_fusion), channel_id=1, source_target_pairs={{0,64},{64,0},{1,65},{65,1},{2,66},{66,2},{3,67},{67,3},{4,68},{68... | collective-permute-start | bytes 2359304 | tf_op jit(solution)/shard_map/ppermute | solution.py:47
  110.9 13.0 %collective-permute-start.5 = (f32[8,128]{1,0:T(8,128)S(1)}, f32[8,128]{1,0:T(8,128)S(1)}, u32[]{:S(2)}, u32[]{:S(2)}) collective-permute-start(f32[8,128]{1,0:T(8,128)S(1)} %broadcast_in_dim.93), channel_id=1, source_target_pairs={{0,128},{128,0},{256,384},{384,256},{512,640},{640,512},{768,896},... | collective-permute-start | bytes 12296 | tf_op jit(solution)/shard_map/ppermute | solution.py:25
  116.2 29.7 %all-to-all-start.3 = ((bf16[64,4,512]{2,1,0:T(4,128)(2,1)}), bf16[64,4,512]{2,1,0:T(4,128)(2,1)S(1)}, u32[]{:S(2)}, u32[]{:S(2)}) async-start(bf16[64,4,512]{2,1,0:T(4,128)(2,1)} %reshape.265), calls=%async_computation.3 | async-start | bytes 524288 | tf_op jit(solution)/shard_map/all_to_all | solution.py:117
  124.6 6.4 %collective-permute-start.6 = (f32[8,128]{1,0:T(8,128)S(1)}, f32[8,128]{1,0:T(8,128)S(1)}, u32[]{:S(2)}, u32[]{:S(2)}) collective-permute-start(f32[8,128]{1,0:T(8,128)S(1)} %broadcast_add_fusion), channel_id=1, source_target_pairs={{0,256},{128,384},{256,0},{384,128},{512,768},{640,896},{768,512},... | collective-permute-start | bytes 12296 | tf_op jit(solution)/shard_map/ppermute | solution.py:25
  131.7 9.4 %collective-permute-start.7 = (f32[8,128]{1,0:T(8,128)S(1)}, f32[8,128]{1,0:T(8,128)S(1)}, u32[]{:S(2)}, u32[]{:S(2)}) collective-permute-start(f32[8,128]{1,0:T(8,128)S(1)} %fusion.69), channel_id=1, source_target_pairs={{0,512},{128,640},{256,768},{384,896},{512,0},{640,128},{768,256},... | collective-permute-start | bytes 12296 | tf_op jit(solution)/shard_map/ppermute | solution.py:25

commit v4 on v3

--- a/solution.py
+++ b/solution.py
@@ -96,11 +96,12 @@
     slot_ids = jnp.arange(most, dtype=jnp.int32)[None, :]
     target = jnp.where(slot_ids < count[:, None], first[:, None] + slot_ids, -1).reshape(-1)
     pack_mat = (jnp.arange(cap, dtype=jnp.int32)[:, None] == target[None, :]).astype(jnp.bfloat16)
+    copy_mat = (jnp.arange(split * cap, dtype=jnp.int32)[:, None] % cap == target[None, :]).astype(jnp.bfloat16)
     packed = jnp.dot(
-        pack_mat, arrived[:, :, :piece].reshape(devices * most, piece), preferred_element_type=jnp.float32
+        copy_mat, arrived[:, :, :piece].reshape(devices * most, piece), preferred_element_type=jnp.float32
     ).astype(jnp.bfloat16)
 
-    rows = copy_to(packed, SHARE, split)
+    rows = lax.all_to_all(packed.reshape(split, cap, piece), SHARE, 0, 0, tiled=True)
     gate = jnp.einsum("kpd,kdf->pf", rows, w_gate.reshape(split, piece, hidden_cols), preferred_element_type=jnp.float32)
     upper = jnp.einsum("kpd,kdf->pf", rows, w_up.reshape(split, piece, hidden_cols), preferred_element_type=jnp.float32)
     hidden = (jax.nn.silu(gate) * upper).astype(jnp.bfloat16)
@@ -118,9 +119,9 @@
     full_out = returned.reshape(experts, split, most, piece).transpose(0, 2, 1, 3).reshape(experts * most, width)
 
     loss = jnp.sum(arrived[:, :, piece:].astype(jnp.float32))
-    loss = lax.psum(loss, "dp_1")
     loss = jnp.broadcast_to(loss, (8, LANES))
     loss = add_partner(loss, "dp_0", 1)
+    loss = lax.psum(loss, "dp_1")
     loss = add_partner(loss, "dp_0", 2)
     loss = add_partner(loss, "dp_0", 4)
     z_loss = loss[0, 0] / (n_dp * devices * rows_dev)

time: 149 us -> 147 us (0.987)
  the two profiles are of different devices: /device:TPU:16 before, /device:TPU:58 now
where the time goes in v4:
time: 147 us
  starting transfers between devices  66.5 us (45%)
  waiting for transfers between devices  56 us (38%)
  matrix products  8.61 us (6%)
  local copies, waits for them, and re-layouts  6.63 us (5%)
  other arithmetic  3.39 us (2%)
  between operations  2.99 us (2%)
  blocking collectives  2.47 us (2%)
    all_to_all x1, waiting for transfers between devices, layer(): arrived = lax.all_to_all(outgoing, TRADE, 0, 0, tiled=True)  23.9 us
    all_to_all x1, starting transfers between devices, layer(): arrived = lax.all_to_all(outgoing, TRADE, 0, 0, tiled=True)  22.3 us
    ppermute x1, waiting for transfers between devices, exchange_down(): other = lax.ppermute(other, 'zp', [(i, 1 - i) for i in range(n_zp)])  15.7 us
    ppermute x3, starting transfers between devices, add_partner(): lax.ppermute(value, axis, [(i, i ^ bit) for i in range(size)])  12 us
    ppermute x3, starting transfers between devices, exchange_down(): part = lax.ppermute(part, 'x', [(i, (i + step) % n_x) for i in range(n_x)])  9.78 us
    ppermute x3, waiting for transfers between devices, add_partner(): lax.ppermute(value, axis, [(i, i ^ bit) for i in range(size)])  9.27 us
    all_to_all x1, starting transfers between devices, layer(): lax.all_to_all(spread.reshape(devices, most, piece), TRADE, 0, 0, tiled=T...  7.18 us
    all_to_all x1, starting transfers between devices, layer(): lax.all_to_all(packed.reshape(split, cap, piece), SHARE, 0, 0, tiled=True)  5.14 us
  transfers between devices with their start and end apart: 12, of which 8 were waited for; matrix products, arithmetic and copies ran while one was open for 6% of the time, Pallas kernels for 0%

profile of v4, /device:TPU:58, one launch (start us, length us, event | category | flops | bytes accessed | tf_op | source)
XLA Modules:
  0.0 146.6 jit_solution(14174200326117992326)
XLA Ops:
  1.9 1.8 %fusion.63 = (f32[128]{0:T(128)S(1)}, f32[128,128]{0,1:T(8,128)S(1)}) fusion(bf16[4096,128]{1,0:T(8,128)(2,1)} %param.7, bf16[1,128,4096]{2,1,0:T(8,128)(2,1)S(1)} %copy-done), kind=kOutput, calls=%fused_computation.127 | convolution fusion | flops 134233984 | bytes 2163200 | tf_op jit(solution)/shard_map/dot_general | solution.py:77
  5.5 22.3 %all-to-all-start = ((bf16[64,4,640]{2,1,0:T(4,128)(2,1)}), bf16[64,4,640]{2,1,0:T(4,128)(2,1)S(1)}, u32[]{:S(2)}, u32[]{:S(2)}) async-start(bf16[64,4,640]{2,1,0:T(4,128)(2,1)} %copy.26), calls=%async_computation | async-start | bytes 655360 | tf_op jit(solution)/shard_map/all_to_all | solution.py:85
  28.3 23.9 %all-to-all-done = bf16[64,4,640]{2,1,0:T(4,128)(2,1)S(1)} async-done(((bf16[64,4,640]{2,1,0:T(4,128)(2,1)}), bf16[64,4,640]{2,1,0:T(4,128)(2,1)S(1)}, u32[]{:S(2)}, u32[]{:S(2)}) %all-to-all-start) | async-done | bytes 327712 | tf_op jit(solution)/shard_map/all_to_all | solution.py:85
  52.3 1.5 convolution_convert_fusion.2
  53.8 5.1 %all-to-all-start.1 = ((bf16[8,128,512]{2,1,0:T(8,128)(2,1)}), bf16[8,128,512]{2,1,0:T(8,128)(2,1)S(1)}, u32[]{:S(2)}, u32[]{:S(2)}) async-start(bf16[8,128,512]{2,1,0:T(8,128)(2,1)} %bitcast.9), calls=%async_computation.1 | async-start | bytes 2097152 | tf_op jit(solution)/shard_map/all_to_all | solution.py:104
  60.0 3.4 %collective-permute-start = (bf16[192,1024]{1,0:T(8,128)(2,1)S(1)}, bf16[192,1024]{1,0:T(8,128)(2,1)S(1)}, u32[]{:S(2)}, u32[]{:S(2)}) collective-permute-start(bf16[192,1024]{1,0:T(8,128)(2,1)S(1)} %pad_maximum_fusion), channel_id=1, source_target_pairs={{0,4},{4,0},{1,5},{5,1},{2,6},{6,2},{3,7},{7,3},{8,12},{12,8},{9,1... | collective-permute-start | bytes 1179656 | tf_op jit(solution)/shard_map/ppermute | solution.py:37
  63.5 15.7 %collective-permute-done = bf16[192,1024]{1,0:T(8,128)(2,1)S(1)} collective-permute-done((bf16[192,1024]{1,0:T(8,128)(2,1)S(1)}, bf16[192,1024]{1,0:T(8,128)(2,1)S(1)}, u32[]{:S(2)}, u32[]{:S(2)}) %collective-permute-start) | collective-permute-done | bytes 393248 | tf_op jit(solution)/shard_map/ppermute | solution.py:37
  80.5 3.9 %collective-permute-start.2 = (bf16[2,192,256]{2,1,0:T(8,128)(2,1)S(1)}, bf16[2,192,256]{2,1,0:T(8,128)(2,1)S(1)}, u32[]{:S(2)}, u32[]{:S(2)}) collective-permute-start(bf16[2,192,256]{2,1,0:T(8,128)(2,1)S(1)} %pad_maximum_fusion.3), channel_id=1, source_target_pairs={{0,2},{1,3},{2,0},{3,1},{4,6},{5,7},{6,4},{7,5},{8,10},{9,11},{10,... | collective-permute-start | bytes 589832 | tf_op jit(solution)/shard_map/ppermute | solution.py:45
  84.5 2.1 %fusion.9 = f32[128,192]{0,1:T(8,128)S(1)} fusion(bf16[8,128,512]{2,1,0:T(8,128)(2,1)S(1)} %all-to-all-done.1, bf16[24,8,8,512]{3,2,1,0:T(8,128)(2,1)} %bitcast.129), kind=kOutput, calls=%fused_computation.15 | convolution fusion | flops 201326592 | bytes 2719744 | tf_op jit(solution)/shard_map/kpd,kdf->pf/dot_general | solution.py:105
  87.9 4.9 %all-to-all-start.2 = ((bf16[8,128,192]{1,2,0:T(8,128)(2,1)}), bf16[8,128,192]{1,2,0:T(8,128)(2,1)S(1)}, u32[]{:S(2)}, u32[]{:S(2)}) async-start(bf16[8,128,192]{1,2,0:T(8,128)(2,1)} %broadcast_in_dim.84), calls=%async_computation.2 | async-start | bytes 786432 | tf_op jit(solution)/shard_map/all_to_all | solution.py:52
  92.8 3.4 %collective-permute-start.1 = (bf16[2,192,256]{2,1,0:T(8,128)(2,1)S(1)}, bf16[2,192,256]{2,1,0:T(8,128)(2,1)S(1)}, u32[]{:S(2)}, u32[]{:S(2)}) collective-permute-start(bf16[2,192,256]{2,1,0:T(8,128)(2,1)S(1)} %pad_maximum_fusion.2), channel_id=1, source_target_pairs={{0,1},{1,2},{2,3},{3,0},{4,5},{5,6},{6,7},{7,4},{8,9},{9,10},{10,1... | collective-permute-start | bytes 589832 | tf_op jit(solution)/shard_map/ppermute | solution.py:45
  96.2 2.5 %collective-permute-start.3 = (bf16[2,192,256]{2,1,0:T(8,128)(2,1)S(1)}, bf16[2,192,256]{2,1,0:T(8,128)(2,1)S(1)}, u32[]{:S(2)}, u32[]{:S(2)}) collective-permute-start(bf16[2,192,256]{2,1,0:T(8,128)(2,1)S(1)} %pad_maximum_fusion.4), channel_id=1, source_target_pairs={{0,3},{1,0},{2,1},{3,2},{4,7},{5,4},{6,5},{7,6},{8,11},{9,8},{10,9... | collective-permute-start | bytes 589832 | tf_op jit(solution)/shard_map/ppermute | solution.py:45
  98.8 1.9 %collective-permute-done.1 = bf16[2,192,256]{2,1,0:T(8,128)(2,1)S(1)} collective-permute-done((bf16[2,192,256]{2,1,0:T(8,128)(2,1)S(1)}, bf16[2,192,256]{2,1,0:T(8,128)(2,1)S(1)}, u32[]{:S(2)}, u32[]{:S(2)}) %collective-permute-start.1) | collective-permute-done | bytes 196640 | tf_op jit(solution)/shard_map/ppermute | solution.py:45
  100.8 3.0 %collective-permute-done.3 = bf16[2,192,256]{2,1,0:T(8,128)(2,1)S(1)} collective-permute-done((bf16[2,192,256]{2,1,0:T(8,128)(2,1)S(1)}, bf16[2,192,256]{2,1,0:T(8,128)(2,1)S(1)}, u32[]{:S(2)}, u32[]{:S(2)}) %collective-permute-start.3) | collective-permute-done | bytes 196640 | tf_op jit(solution)/shard_map/ppermute | solution.py:45
  103.8 1.9 %collective-permute-start.4 = (bf16[8,192,256]{2,1,0:T(8,128)(2,1)S(1)}, bf16[8,192,256]{2,1,0:T(8,128)(2,1)S(1)}, u32[]{:S(2)}, u32[]{:S(2)}) collective-permute-start(bf16[8,192,256]{2,1,0:T(8,128)(2,1)S(1)} %constant_dynamic-update-slice_fusion), channel_id=1, source_target_pairs={{0,64},{64,0},{1,65},{65,1},{2,66},{66,2},{3,67},{67,3},{4,68},{68... | collective-permute-start | bytes 2359304 | tf_op jit(solution)/shard_map/ppermute | solution.py:47
  105.8 2.2 %collective-permute-done.4 = bf16[8,192,256]{2,1,0:T(8,128)(2,1)S(1)} collective-permute-done((bf16[8,192,256]{2,1,0:T(8,128)(2,1)S(1)}, bf16[8,192,256]{2,1,0:T(8,128)(2,1)S(1)}, u32[]{:S(2)}, u32[]{:S(2)}) %collective-permute-start.4) | collective-permute-done | bytes 786464 | tf_op jit(solution)/shard_map/ppermute | solution.py:47
  109.7 7.2 %all-to-all-start.3 = ((bf16[64,4,512]{2,1,0:T(4,128)(2,1)}), bf16[64,4,512]{2,1,0:T(4,128)(2,1)S(1)}, u32[]{:S(2)}, u32[]{:S(2)}) async-start(bf16[64,4,512]{2,1,0:T(4,128)(2,1)} %reshape.283), calls=%async_computation.3 | async-start | bytes 524288 | tf_op jit(solution)/shard_map/all_to_all | solution.py:118
  118.2 3.3 %collective-permute-start.5 = (f32[8,128]{1,0:T(8,128)S(1)}, f32[8,128]{1,0:T(8,128)S(1)}, u32[]{:S(2)}, u32[]{:S(2)}) collective-permute-start(f32[8,128]{1,0:T(8,128)S(1)} %broadcast_in_dim.87), channel_id=1, source_target_pairs={{0,128},{128,0},{256,384},{384,256},{512,640},{640,512},{768,896},... | collective-permute-start | bytes 12296 | tf_op jit(solution)/shard_map/ppermute | solution.py:25
  121.5 2.2 %collective-permute-done.5 = f32[8,128]{1,0:T(8,128)S(1)} collective-permute-done((f32[8,128]{1,0:T(8,128)S(1)}, f32[8,128]{1,0:T(8,128)S(1)}, u32[]{:S(2)}, u32[]{:S(2)}) %collective-permute-start.5) | collective-permute-done | bytes 4128 | tf_op jit(solution)/shard_map/ppermute | solution.py:25
  124.4 2.5 %psum.7 = f32[8,128]{1,0:T(8,128)S(1)} all-reduce(f32[8,128]{1,0:T(8,128)S(1)} %broadcast_add_fusion), channel_id=1, replica_groups=mesh['dp_0'=8,'dp_1'=2,'ez'=8,'zp'=2,'x'=4] {'dp_1'}, use_global_device_ids=true, to_apply=%region_9.10 | all-reduce | flops 1024 | bytes 8192 | tf_op jit(solution)/shard_map/psum | solution.py:124
  126.9 4.0 %collective-permute-start.6 = (f32[8,128]{1,0:T(8,128)S(1)}, f32[8,128]{1,0:T(8,128)S(1)}, u32[]{:S(2)}, u32[]{:S(2)}) collective-permute-start(f32[8,128]{1,0:T(8,128)S(1)} %psum.7), channel_id=1, source_target_pairs={{0,256},{128,384},{256,0},{384,128},{512,768},{640,896},{768,512},... | collective-permute-start | bytes 12296 | tf_op jit(solution)/shard_map/ppermute | solution.py:25
  130.9 2.4 %collective-permute-done.6 = f32[8,128]{1,0:T(8,128)S(1)} collective-permute-done((f32[8,128]{1,0:T(8,128)S(1)}, f32[8,128]{1,0:T(8,128)S(1)}, u32[]{:S(2)}, u32[]{:S(2)}) %collective-permute-start.6) | collective-permute-done | bytes 4128 | tf_op jit(solution)/shard_map/ppermute | solution.py:25
  133.3 4.7 %collective-permute-start.7 = (f32[8,128]{1,0:T(8,128)S(1)}, f32[8,128]{1,0:T(8,128)S(1)}, u32[]{:S(2)}, u32[]{:S(2)}) collective-permute-start(f32[8,128]{1,0:T(8,128)S(1)} %add.313), channel_id=1, source_target_pairs={{0,512},{128,640},{256,768},{384,896},{512,0},{640,128},{768,256},... | collective-permute-start | bytes 12296 | tf_op jit(solution)/shard_map/ppermute | solution.py:25
  138.0 4.7 %collective-permute-done.7 = f32[8,128]{1,0:T(8,128)S(1)} collective-permute-done((f32[8,128]{1,0:T(8,128)S(1)}, f32[8,128]{1,0:T(8,128)S(1)}, u32[]{:S(2)}, u32[]{:S(2)}) %collective-permute-start.7) | collective-permute-done | bytes 4128 | tf_op jit(solution)/shard_map/ppermute | solution.py:25
  (67 shorter events, 13.3 us)
Async XLA Ops:
  0.6 1.2 copy-start
  0.6 3.1 %copy-start.1 = (s32[1,8,128]{2,1,0:T(8,128)S(1)}, s32[1,8,128]{2,1,0:T(8,128)}, u32[]{:S(2)}) copy-start(s32[1,8,128]{2,1,0:T(8,128)} %param.8) | copy-start | bytes 12292
  5.5 46.6 %all-to-all-start = ((bf16[64,4,640]{2,1,0:T(4,128)(2,1)}), bf16[64,4,640]{2,1,0:T(4,128)(2,1)S(1)}, u32[]{:S(2)}, u32[]{:S(2)}) async-start(bf16[64,4,640]{2,1,0:T(4,128)(2,1)} %copy.26), calls=%async_computation | async-start | bytes 655360 | tf_op jit(solution)/shard_map/all_to_all | solution.py:85
  53.8 30.7 %all-to-all-start.1 = ((bf16[8,128,512]{2,1,0:T(8,128)(2,1)}), bf16[8,128,512]{2,1,0:T(8,128)(2,1)S(1)}, u32[]{:S(2)}, u32[]{:S(2)}) async-start(bf16[8,128,512]{2,1,0:T(8,128)(2,1)} %bitcast.9), calls=%async_computation.1 | async-start | bytes 2097152 | tf_op jit(solution)/shard_map/all_to_all | solution.py:104
  60.0 19.2 %collective-permute-start = (bf16[192,1024]{1,0:T(8,128)(2,1)S(1)}, bf16[192,1024]{1,0:T(8,128)(2,1)S(1)}, u32[]{:S(2)}, u32[]{:S(2)}) collective-permute-start(bf16[192,1024]{1,0:T(8,128)(2,1)S(1)} %pad_maximum_fusion), channel_id=1, source_target_pairs={{0,4},{4,0},{1,5},{5,1},{2,6},{6,2},{3,7},{7,3},{8,12},{12,8},{9,1... | collective-permute-start | bytes 1179656 | tf_op jit(solution)/shard_map/ppermute | solution.py:37
  80.5 20.2 %collective-permute-start.2 = (bf16[2,192,256]{2,1,0:T(8,128)(2,1)S(1)}, bf16[2,192,256]{2,1,0:T(8,128)(2,1)S(1)}, u32[]{:S(2)}, u32[]{:S(2)}) collective-permute-start(bf16[2,192,256]{2,1,0:T(8,128)(2,1)S(1)} %pad_maximum_fusion.3), channel_id=1, source_target_pairs={{0,2},{1,3},{2,0},{3,1},{4,6},{5,7},{6,4},{7,5},{8,10},{9,11},{10,... | collective-permute-start | bytes 589832 | tf_op jit(solution)/shard_map/ppermute | solution.py:45
  84.4 2.1 %copy-start.2 = (bf16[4096,192]{0,1:T(8,128)(2,1)S(1)}, bf16[4096,192]{0,1:T(8,128)(2,1)}, u32[]{:S(2)}) copy-start(bf16[4096,192]{0,1:T(8,128)(2,1)} %param.10) | copy-start | bytes 4718596
  87.9 20.1 %all-to-all-start.2 = ((bf16[8,128,192]{1,2,0:T(8,128)(2,1)}), bf16[8,128,192]{1,2,0:T(8,128)(2,1)S(1)}, u32[]{:S(2)}, u32[]{:S(2)}) async-start(bf16[8,128,192]{1,2,0:T(8,128)(2,1)} %broadcast_in_dim.84), calls=%async_computation.2 | async-start | bytes 786432 | tf_op jit(solution)/shard_map/all_to_all | solution.py:52
  92.8 7.9 %collective-permute-start.1 = (bf16[2,192,256]{2,1,0:T(8,128)(2,1)S(1)}, bf16[2,192,256]{2,1,0:T(8,128)(2,1)S(1)}, u32[]{:S(2)}, u32[]{:S(2)}) collective-permute-start(bf16[2,192,256]{2,1,0:T(8,128)(2,1)S(1)} %pad_maximum_fusion.2), channel_id=1, source_target_pairs={{0,1},{1,2},{2,3},{3,0},{4,5},{5,6},{6,7},{7,4},{8,9},{9,10},{10,1... | collective-permute-start | bytes 589832 | tf_op jit(solution)/shard_map/ppermute | solution.py:45
  96.2 7.6 %collective-permute-start.3 = (bf16[2,192,256]{2,1,0:T(8,128)(2,1)S(1)}, bf16[2,192,256]{2,1,0:T(8,128)(2,1)S(1)}, u32[]{:S(2)}, u32[]{:S(2)}) collective-permute-start(bf16[2,192,256]{2,1,0:T(8,128)(2,1)S(1)} %pad_maximum_fusion.4), channel_id=1, source_target_pairs={{0,3},{1,0},{2,1},{3,2},{4,7},{5,4},{6,5},{7,6},{8,11},{9,8},{10,9... | collective-permute-start | bytes 589832 | tf_op jit(solution)/shard_map/ppermute | solution.py:45
  103.8 4.2 %collective-permute-start.4 = (bf16[8,192,256]{2,1,0:T(8,128)(2,1)S(1)}, bf16[8,192,256]{2,1,0:T(8,128)(2,1)S(1)}, u32[]{:S(2)}, u32[]{:S(2)}) collective-permute-start(bf16[8,192,256]{2,1,0:T(8,128)(2,1)S(1)} %constant_dynamic-update-slice_fusion), channel_id=1, source_target_pairs={{0,64},{64,0},{1,65},{65,1},{2,66},{66,2},{3,67},{67,3},{4,68},{68... | collective-permute-start | bytes 2359304 | tf_op jit(solution)/shard_map/ppermute | solution.py:47
  109.7 34.1 %all-to-all-start.3 = ((bf16[64,4,512]{2,1,0:T(4,128)(2,1)}), bf16[64,4,512]{2,1,0:T(4,128)(2,1)S(1)}, u32[]{:S(2)}, u32[]{:S(2)}) async-start(bf16[64,4,512]{2,1,0:T(4,128)(2,1)} %reshape.283), calls=%async_computation.3 | async-start | bytes 524288 | tf_op jit(solution)/shard_map/all_to_all | solution.py:118
  118.2 5.5 %collective-permute-start.5 = (f32[8,128]{1,0:T(8,128)S(1)}, f32[8,128]{1,0:T(8,128)S(1)}, u32[]{:S(2)}, u32[]{:S(2)}) collective-permute-start(f32[8,128]{1,0:T(8,128)S(1)} %broadcast_in_dim.87), channel_id=1, source_target_pairs={{0,128},{128,0},{256,384},{384,256},{512,640},{640,512},{768,896},... | collective-permute-start | bytes 12296 | tf_op jit(solution)/shard_map/ppermute | solution.py:25
  126.9 6.4 %collective-permute-start.6 = (f32[8,128]{1,0:T(8,128)S(1)}, f32[8,128]{1,0:T(8,128)S(1)}, u32[]{:S(2)}, u32[]{:S(2)}) collective-permute-start(f32[8,128]{1,0:T(8,128)S(1)} %psum.7), channel_id=1, source_target_pairs={{0,256},{128,384},{256,0},{384,128},{512,768},{640,896},{768,512},... | collective-permute-start | bytes 12296 | tf_op jit(solution)/shard_map/ppermute | solution.py:25
  133.3 9.4 %collective-permute-start.7 = (f32[8,128]{1,0:T(8,128)S(1)}, f32[8,128]{1,0:T(8,128)S(1)}, u32[]{:S(2)}, u32[]{:S(2)}) collective-permute-start(f32[8,128]{1,0:T(8,128)S(1)} %add.313), channel_id=1, source_target_pairs={{0,512},{128,640},{256,768},{384,896},{512,0},{640,128},{768,256},... | collective-permute-start | bytes 12296 | tf_op jit(solution)/shard_map/ppermute | solution.py:25

commit v5 on v3

--- a/solution.py
+++ b/solution.py
@@ -104,11 +104,12 @@
     gate = jnp.einsum("kpd,kdf->pf", rows, w_gate.reshape(split, piece, hidden_cols), preferred_element_type=jnp.float32)
     upper = jnp.einsum("kpd,kdf->pf", rows, w_up.reshape(split, piece, hidden_cols), preferred_element_type=jnp.float32)
     hidden = (jax.nn.silu(gate) * upper).astype(jnp.bfloat16)
+    hidden, down_theirs, first_core = lax.optimization_barrier((hidden, down_theirs, core == 0))
     hidden = copy_to(hidden, SHARE, split)
     out_mine = jnp.einsum("kpf,kfd->pd", hidden, down_mine, preferred_element_type=jnp.float32).astype(jnp.bfloat16)
     out_theirs = jnp.einsum("kpf,kfd->pd", hidden, down_theirs, preferred_element_type=jnp.float32).astype(jnp.bfloat16)
-    low = jnp.where(core == 0, out_mine, out_theirs)
-    high = jnp.where(core == 0, out_theirs, out_mine)
+    low = jnp.where(first_core, out_mine, out_theirs)
+    high = jnp.where(first_core, out_theirs, out_mine)
     expert_out = jnp.concatenate([low, high], axis=1)
     spread = lax.dot_general(
         pack_mat, expert_out, (((0,), (0,)), ((), ())), preferred_element_type=jnp.float32
@@ -118,9 +119,9 @@
     full_out = returned.reshape(experts, split, most, piece).transpose(0, 2, 1, 3).reshape(experts * most, width)
 
     loss = jnp.sum(arrived[:, :, piece:].astype(jnp.float32))
-    loss = lax.psum(loss, "dp_1")
     loss = jnp.broadcast_to(loss, (8, LANES))
     loss = add_partner(loss, "dp_0", 1)
+    loss = lax.psum(loss, "dp_1")
     loss = add_partner(loss, "dp_0", 2)
     loss = add_partner(loss, "dp_0", 4)
     z_loss = loss[0, 0] / (n_dp * devices * rows_dev)

time: 149 us -> 155 us (1.040)
  the two profiles are of different devices: /device:TPU:16 before, /device:TPU:58 now
where the time goes in v5:
time: 155 us; the launch traced here: 154 us
  starting transfers between devices  67.6 us (44%)
  waiting for transfers between devices  61.6 us (40%)
  matrix products  8.91 us (6%)
  local copies, waits for them, and re-layouts  6.68 us (4%)
  other arithmetic  3.38 us (2%)
  between operations  3 us (2%)
  blocking collectives  2.47 us (2%)
    all_to_all x1, waiting for transfers between devices, layer(): arrived = lax.all_to_all(outgoing, TRADE, 0, 0, tiled=True)  23.9 us
    all_to_all x1, starting transfers between devices, layer(): arrived = lax.all_to_all(outgoing, TRADE, 0, 0, tiled=True)  22.3 us
    ppermute x1, waiting for transfers between devices, exchange_down(): other = lax.ppermute(other, 'zp', [(i, 1 - i) for i in range(n_zp)])  16.8 us
    ppermute x3, starting transfers between devices, add_partner(): lax.ppermute(value, axis, [(i, i ^ bit) for i in range(size)])  12 us
    ppermute x3, starting transfers between devices, exchange_down(): part = lax.ppermute(part, 'x', [(i, (i + step) % n_x) for i in range(n_x)])  10.4 us
    all_to_all x2, starting transfers between devices, copy_to(): lax.all_to_all(jnp.broadcast_to(value[None], (count,) + value.shape), axe...  10.4 us
    ppermute x3, waiting for transfers between devices, add_partner(): lax.ppermute(value, axis, [(i, i ^ bit) for i in range(size)])  9.27 us
    all_to_all x1, starting transfers between devices, layer(): lax.all_to_all(spread.reshape(devices, most, piece), TRADE, 0, 0, tiled=T...  7.34 us
  transfers between devices with their start and end apart: 12, of which 8 were waited for; matrix products, arithmetic and copies ran while one was open for 6% of the time, Pallas kernels for 0%

profile of v5, /device:TPU:58, one launch (start us, length us, event | category | flops | bytes accessed | tf_op | source)
XLA Modules:
  0.0 153.7 jit_solution(4739184735900195419)
XLA Ops:
  1.9 1.8 %fusion.58 = (f32[128]{0:T(128)S(1)}, f32[128,128]{0,1:T(8,128)S(1)}) fusion(bf16[4096,128]{1,0:T(8,128)(2,1)} %param.7, bf16[1,128,4096]{2,1,0:T(8,128)(2,1)S(1)} %copy-done), kind=kOutput, calls=%fused_computation.120 | convolution fusion | flops 134233984 | bytes 2163200 | tf_op jit(solution)/shard_map/dot_general | solution.py:77
  5.5 22.3 %all-to-all-start = ((bf16[64,4,640]{2,1,0:T(4,128)(2,1)}), bf16[64,4,640]{2,1,0:T(4,128)(2,1)S(1)}, u32[]{:S(2)}, u32[]{:S(2)}) async-start(bf16[64,4,640]{2,1,0:T(4,128)(2,1)} %copy.26), calls=%async_computation | async-start | bytes 655360 | tf_op jit(solution)/shard_map/all_to_all | solution.py:85
  28.3 23.9 %all-to-all-done = bf16[64,4,640]{2,1,0:T(4,128)(2,1)S(1)} async-done(((bf16[64,4,640]{2,1,0:T(4,128)(2,1)}), bf16[64,4,640]{2,1,0:T(4,128)(2,1)S(1)}, u32[]{:S(2)}, u32[]{:S(2)}) %all-to-all-start) | async-done | bytes 327712 | tf_op jit(solution)/shard_map/all_to_all | solution.py:85
  53.6 5.1 %all-to-all-start.1 = ((bf16[8,128,512]{2,1,0:T(8,128)(2,1)}), bf16[8,128,512]{2,1,0:T(8,128)(2,1)}, u32[]{:S(2)}, u32[]{:S(2)}) async-start(bf16[8,128,512]{2,1,0:T(8,128)(2,1)} %broadcast_in_dim.89), calls=%async_computation.1 | async-start | bytes 2097152 | tf_op jit(solution)/shard_map/all_to_all | solution.py:52
  58.8 3.4 %collective-permute-start = (bf16[192,1024]{1,0:T(8,128)(2,1)S(1)}, bf16[192,1024]{1,0:T(8,128)(2,1)}, u32[]{:S(2)}, u32[]{:S(2)}) collective-permute-start(bf16[192,1024]{1,0:T(8,128)(2,1)S(1)} %pad_maximum_fusion), channel_id=1, source_target_pairs={{0,4},{4,0},{1,5},{5,1},{2,6},{6,2},{3,7},{7,3},{8,12},{12,8},{9,1... | collective-permute-start | bytes 1179656 | tf_op jit(solution)/shard_map/ppermute | solution.py:37
  62.3 16.8 %collective-permute-done = bf16[192,1024]{1,0:T(8,128)(2,1)} collective-permute-done((bf16[192,1024]{1,0:T(8,128)(2,1)S(1)}, bf16[192,1024]{1,0:T(8,128)(2,1)}, u32[]{:S(2)}, u32[]{:S(2)}) %collective-permute-start) | collective-permute-done | bytes 393248 | tf_op jit(solution)/shard_map/ppermute | solution.py:37
  80.4 3.4 %collective-permute-start.1 = (bf16[2,192,256]{2,1,0:T(8,128)(2,1)S(1)}, bf16[2,192,256]{2,1,0:T(8,128)(2,1)S(1)}, u32[]{:S(2)}, u32[]{:S(2)}) collective-permute-start(bf16[2,192,256]{2,1,0:T(8,128)(2,1)S(1)} %pad_maximum_fusion.2), channel_id=1, source_target_pairs={{0,1},{1,2},{2,3},{3,0},{4,5},{5,6},{6,7},{7,4},{8,9},{9,10},{10,1... | collective-permute-start | bytes 589832 | tf_op jit(solution)/shard_map/ppermute | solution.py:45
  83.8 3.0 %collective-permute-start.2 = (bf16[2,192,256]{2,1,0:T(8,128)(2,1)S(1)}, bf16[2,192,256]{2,1,0:T(8,128)(2,1)S(1)}, u32[]{:S(2)}, u32[]{:S(2)}) collective-permute-start(bf16[2,192,256]{2,1,0:T(8,128)(2,1)S(1)} %pad_maximum_fusion.3), channel_id=1, source_target_pairs={{0,2},{1,3},{2,0},{3,1},{4,6},{5,7},{6,4},{7,5},{8,10},{9,11},{10,... | collective-permute-start | bytes 589832 | tf_op jit(solution)/shard_map/ppermute | solution.py:45
  86.9 4.0 %collective-permute-start.3 = (bf16[2,192,256]{2,1,0:T(8,128)(2,1)S(1)}, bf16[2,192,256]{2,1,0:T(8,128)(2,1)S(1)}, u32[]{:S(2)}, u32[]{:S(2)}) collective-permute-start(bf16[2,192,256]{2,1,0:T(8,128)(2,1)S(1)} %pad_maximum_fusion.4), channel_id=1, source_target_pairs={{0,3},{1,0},{2,1},{3,2},{4,7},{5,4},{6,5},{7,6},{8,11},{9,8},{10,9... | collective-permute-start | bytes 589832 | tf_op jit(solution)/shard_map/ppermute | solution.py:45
  91.0 2.5 %collective-permute-done.2 = bf16[2,192,256]{2,1,0:T(8,128)(2,1)S(1)} collective-permute-done((bf16[2,192,256]{2,1,0:T(8,128)(2,1)S(1)}, bf16[2,192,256]{2,1,0:T(8,128)(2,1)S(1)}, u32[]{:S(2)}, u32[]{:S(2)}) %collective-permute-start.2) | collective-permute-done | bytes 196640 | tf_op jit(solution)/shard_map/ppermute | solution.py:45
  93.5 2.0 %collective-permute-done.3 = bf16[2,192,256]{2,1,0:T(8,128)(2,1)S(1)} collective-permute-done((bf16[2,192,256]{2,1,0:T(8,128)(2,1)S(1)}, bf16[2,192,256]{2,1,0:T(8,128)(2,1)S(1)}, u32[]{:S(2)}, u32[]{:S(2)}) %collective-permute-start.3) | collective-permute-done | bytes 196640 | tf_op jit(solution)/shard_map/ppermute | solution.py:45
  95.5 1.9 %collective-permute-start.4 = (bf16[8,192,256]{2,1,0:T(8,128)(2,1)S(1)}, bf16[8,192,256]{2,1,0:T(8,128)(2,1)S(1)}, u32[]{:S(2)}, u32[]{:S(2)}) collective-permute-start(bf16[8,192,256]{2,1,0:T(8,128)(2,1)S(1)} %constant_dynamic-update-slice_fusion), channel_id=1, source_target_pairs={{0,64},{64,0},{1,65},{65,1},{2,66},{66,2},{3,67},{67,3},{4,68},{68... | collective-permute-start | bytes 2359304 | tf_op jit(solution)/shard_map/ppermute | solution.py:47
  97.4 2.4 %fusion.9 = f32[128,192]{0,1:T(8,128)S(1)} fusion(bf16[8,128,512]{2,1,0:T(8,128)(2,1)} %all-to-all-done.1, bf16[24,8,8,512]{3,2,1,0:T(8,128)(2,1)} %bitcast.128), kind=kOutput, calls=%fused_computation.15 | convolution fusion | flops 201326592 | bytes 2719744 | tf_op jit(solution)/shard_map/kpd,kdf->pf/dot_general | solution.py:104
  99.9 1.8 %fusion.18 = bf16[128,192]{0,1:T(8,128)(2,1)S(1)} fusion(bf16[8,128,512]{2,1,0:T(8,128)(2,1)} %all-to-all-done.1, bf16[24,8,8,512]{3,2,1,0:T(8,128)(2,1)S(1)} %bitcast.129, f32[128,192]{0,1:T(8,128)S(1)} %fusion.9), kind=kOutput, calls=%fused_computation.18 | convolution fusion | flops 201474048 | bytes 2768896 | tf_op jit(solution)/shard_map/kpd,kdf->pf/dot_general | solution.py:105
  102.5 5.2 %all-to-all-start.2 = ((bf16[8,128,192]{1,2,0:T(8,128)(2,1)}), bf16[8,128,192]{1,2,0:T(8,128)(2,1)S(1)}, u32[]{:S(2)}, u32[]{:S(2)}) async-start(bf16[8,128,192]{1,2,0:T(8,128)(2,1)} %broadcast_in_dim.91), calls=%async_computation.2 | async-start | bytes 786432 | tf_op jit(solution)/shard_map/all_to_all | solution.py:52
  107.8 7.2 %all-to-all-done.2 = bf16[8,128,192]{1,2,0:T(8,128)(2,1)S(1)} async-done(((bf16[8,128,192]{1,2,0:T(8,128)(2,1)}), bf16[8,128,192]{1,2,0:T(8,128)(2,1)S(1)}, u32[]{:S(2)}, u32[]{:S(2)}) %all-to-all-start.2) | async-done | bytes 393248 | tf_op jit(solution)/shard_map/all_to_all | solution.py:52
  116.7 7.3 %all-to-all-start.3 = ((bf16[64,4,512]{2,1,0:T(4,128)(2,1)}), bf16[64,4,512]{2,1,0:T(4,128)(2,1)S(1)}, u32[]{:S(2)}, u32[]{:S(2)}) async-start(bf16[64,4,512]{2,1,0:T(4,128)(2,1)} %reshape.265), calls=%async_computation.3 | async-start | bytes 524288 | tf_op jit(solution)/shard_map/all_to_all | solution.py:118
  125.3 3.3 %collective-permute-start.5 = (f32[8,128]{1,0:T(8,128)S(1)}, f32[8,128]{1,0:T(8,128)S(1)}, u32[]{:S(2)}, u32[]{:S(2)}) collective-permute-start(f32[8,128]{1,0:T(8,128)S(1)} %broadcast_in_dim.93), channel_id=1, source_target_pairs={{0,128},{128,0},{256,384},{384,256},{512,640},{640,512},{768,896},... | collective-permute-start | bytes 12296 | tf_op jit(solution)/shard_map/ppermute | solution.py:25
  128.6 2.2 %collective-permute-done.5 = f32[8,128]{1,0:T(8,128)S(1)} collective-permute-done((f32[8,128]{1,0:T(8,128)S(1)}, f32[8,128]{1,0:T(8,128)S(1)}, u32[]{:S(2)}, u32[]{:S(2)}) %collective-permute-start.5) | collective-permute-done | bytes 4128 | tf_op jit(solution)/shard_map/ppermute | solution.py:25
  131.5 2.5 %psum.7 = f32[8,128]{1,0:T(8,128)S(1)} all-reduce(f32[8,128]{1,0:T(8,128)S(1)} %broadcast_add_fusion), channel_id=1, replica_groups=mesh['dp_0'=8,'dp_1'=2,'ez'=8,'zp'=2,'x'=4] {'dp_1'}, use_global_device_ids=true, to_apply=%region_9.10 | all-reduce | flops 1024 | bytes 8192 | tf_op jit(solution)/shard_map/psum | solution.py:124
  134.0 4.0 %collective-permute-start.6 = (f32[8,128]{1,0:T(8,128)S(1)}, f32[8,128]{1,0:T(8,128)S(1)}, u32[]{:S(2)}, u32[]{:S(2)}) collective-permute-start(f32[8,128]{1,0:T(8,128)S(1)} %psum.7), channel_id=1, source_target_pairs={{0,256},{128,384},{256,0},{384,128},{512,768},{640,896},{768,512},... | collective-permute-start | bytes 12296 | tf_op jit(solution)/shard_map/ppermute | solution.py:25
  138.0 2.4 %collective-permute-done.6 = f32[8,128]{1,0:T(8,128)S(1)} collective-permute-done((f32[8,128]{1,0:T(8,128)S(1)}, f32[8,128]{1,0:T(8,128)S(1)}, u32[]{:S(2)}, u32[]{:S(2)}) %collective-permute-start.6) | collective-permute-done | bytes 4128 | tf_op jit(solution)/shard_map/ppermute | solution.py:25
  140.4 4.7 %collective-permute-start.7 = (f32[8,128]{1,0:T(8,128)S(1)}, f32[8,128]{1,0:T(8,128)S(1)}, u32[]{:S(2)}, u32[]{:S(2)}) collective-permute-start(f32[8,128]{1,0:T(8,128)S(1)} %add.301), channel_id=1, source_target_pairs={{0,512},{128,640},{256,768},{384,896},{512,0},{640,128},{768,256},... | collective-permute-start | bytes 12296 | tf_op jit(solution)/shard_map/ppermute | solution.py:25
  145.1 4.7 %collective-permute-done.7 = f32[8,128]{1,0:T(8,128)S(1)} collective-permute-done((f32[8,128]{1,0:T(8,128)S(1)}, f32[8,128]{1,0:T(8,128)S(1)}, u32[]{:S(2)}, u32[]{:S(2)}) %collective-permute-start.7) | collective-permute-done | bytes 4128 | tf_op jit(solution)/shard_map/ppermute | solution.py:25
  (69 shorter events, 13.0 us)
Async XLA Ops:
  0.6 1.2 copy-start
  0.6 3.1 %copy-start.2 = (s32[1,8,128]{2,1,0:T(8,128)S(1)}, s32[1,8,128]{2,1,0:T(8,128)}, u32[]{:S(2)}) copy-start(s32[1,8,128]{2,1,0:T(8,128)} %param.8) | copy-start | bytes 12292
  5.5 46.6 %all-to-all-start = ((bf16[64,4,640]{2,1,0:T(4,128)(2,1)}), bf16[64,4,640]{2,1,0:T(4,128)(2,1)S(1)}, u32[]{:S(2)}, u32[]{:S(2)}) async-start(bf16[64,4,640]{2,1,0:T(4,128)(2,1)} %copy.26), calls=%async_computation | async-start | bytes 655360 | tf_op jit(solution)/shard_map/all_to_all | solution.py:85
  52.5 6.2 %copy-start.1 = (bf16[192,4096]{1,0:T(8,128)(2,1)S(1)}, bf16[192,4096]{1,0:T(8,128)(2,1)}, u32[]{:S(2)}) copy-start(bf16[192,4096]{1,0:T(8,128)(2,1)} %param.11) | copy-start | bytes 4718596
  53.6 43.8 %all-to-all-start.1 = ((bf16[8,128,512]{2,1,0:T(8,128)(2,1)}), bf16[8,128,512]{2,1,0:T(8,128)(2,1)}, u32[]{:S(2)}, u32[]{:S(2)}) async-start(bf16[8,128,512]{2,1,0:T(8,128)(2,1)} %broadcast_in_dim.89), calls=%async_computation.1 | async-start | bytes 2097152 | tf_op jit(solution)/shard_map/all_to_all | solution.py:52
  58.8 20.3 %collective-permute-start = (bf16[192,1024]{1,0:T(8,128)(2,1)S(1)}, bf16[192,1024]{1,0:T(8,128)(2,1)}, u32[]{:S(2)}, u32[]{:S(2)}) collective-permute-start(bf16[192,1024]{1,0:T(8,128)(2,1)S(1)} %pad_maximum_fusion), channel_id=1, source_target_pairs={{0,4},{4,0},{1,5},{5,1},{2,6},{6,2},{3,7},{7,3},{8,12},{12,8},{9,1... | collective-permute-start | bytes 1179656 | tf_op jit(solution)/shard_map/ppermute | solution.py:37
  80.4 10.6 %collective-permute-start.1 = (bf16[2,192,256]{2,1,0:T(8,128)(2,1)S(1)}, bf16[2,192,256]{2,1,0:T(8,128)(2,1)S(1)}, u32[]{:S(2)}, u32[]{:S(2)}) collective-permute-start(bf16[2,192,256]{2,1,0:T(8,128)(2,1)S(1)} %pad_maximum_fusion.2), channel_id=1, source_target_pairs={{0,1},{1,2},{2,3},{3,0},{4,5},{5,6},{6,7},{7,4},{8,9},{9,10},{10,1... | collective-permute-start | bytes 589832 | tf_op jit(solution)/shard_map/ppermute | solution.py:45
  83.8 9.6 %collective-permute-start.2 = (bf16[2,192,256]{2,1,0:T(8,128)(2,1)S(1)}, bf16[2,192,256]{2,1,0:T(8,128)(2,1)S(1)}, u32[]{:S(2)}, u32[]{:S(2)}) collective-permute-start(bf16[2,192,256]{2,1,0:T(8,128)(2,1)S(1)} %pad_maximum_fusion.3), channel_id=1, source_target_pairs={{0,2},{1,3},{2,0},{3,1},{4,6},{5,7},{6,4},{7,5},{8,10},{9,11},{10,... | collective-permute-start | bytes 589832 | tf_op jit(solution)/shard_map/ppermute | solution.py:45
  86.9 8.6 %collective-permute-start.3 = (bf16[2,192,256]{2,1,0:T(8,128)(2,1)S(1)}, bf16[2,192,256]{2,1,0:T(8,128)(2,1)S(1)}, u32[]{:S(2)}, u32[]{:S(2)}) collective-permute-start(bf16[2,192,256]{2,1,0:T(8,128)(2,1)S(1)} %pad_maximum_fusion.4), channel_id=1, source_target_pairs={{0,3},{1,0},{2,1},{3,2},{4,7},{5,4},{6,5},{7,6},{8,11},{9,8},{10,9... | collective-permute-start | bytes 589832 | tf_op jit(solution)/shard_map/ppermute | solution.py:45
  95.5 6.2 %collective-permute-start.4 = (bf16[8,192,256]{2,1,0:T(8,128)(2,1)S(1)}, bf16[8,192,256]{2,1,0:T(8,128)(2,1)S(1)}, u32[]{:S(2)}, u32[]{:S(2)}) collective-permute-start(bf16[8,192,256]{2,1,0:T(8,128)(2,1)S(1)} %constant_dynamic-update-slice_fusion), channel_id=1, source_target_pairs={{0,64},{64,0},{1,65},{65,1},{2,66},{66,2},{3,67},{67,3},{4,68},{68... | collective-permute-start | bytes 2359304 | tf_op jit(solution)/shard_map/ppermute | solution.py:47
  97.4 2.4 %copy-start.3 = (bf16[4096,192]{0,1:T(8,128)(2,1)S(1)}, bf16[4096,192]{0,1:T(8,128)(2,1)}, u32[]{:S(2)}) copy-start(bf16[4096,192]{0,1:T(8,128)(2,1)} %param.10) | copy-start | bytes 4718596
  102.5 12.4 %all-to-all-start.2 = ((bf16[8,128,192]{1,2,0:T(8,128)(2,1)}), bf16[8,128,192]{1,2,0:T(8,128)(2,1)S(1)}, u32[]{:S(2)}, u32[]{:S(2)}) async-start(bf16[8,128,192]{1,2,0:T(8,128)(2,1)} %broadcast_in_dim.91), calls=%async_computation.2 | async-start | bytes 786432 | tf_op jit(solution)/shard_map/all_to_all | solution.py:52
  116.7 34.3 %all-to-all-start.3 = ((bf16[64,4,512]{2,1,0:T(4,128)(2,1)}), bf16[64,4,512]{2,1,0:T(4,128)(2,1)S(1)}, u32[]{:S(2)}, u32[]{:S(2)}) async-start(bf16[64,4,512]{2,1,0:T(4,128)(2,1)} %reshape.265), calls=%async_computation.3 | async-start | bytes 524288 | tf_op jit(solution)/shard_map/all_to_all | solution.py:118
  125.3 5.5 %collective-permute-start.5 = (f32[8,128]{1,0:T(8,128)S(1)}, f32[8,128]{1,0:T(8,128)S(1)}, u32[]{:S(2)}, u32[]{:S(2)}) collective-permute-start(f32[8,128]{1,0:T(8,128)S(1)} %broadcast_in_dim.93), channel_id=1, source_target_pairs={{0,128},{128,0},{256,384},{384,256},{512,640},{640,512},{768,896},... | collective-permute-start | bytes 12296 | tf_op jit(solution)/shard_map/ppermute | solution.py:25
  134.0 6.4 %collective-permute-start.6 = (f32[8,128]{1,0:T(8,128)S(1)}, f32[8,128]{1,0:T(8,128)S(1)}, u32[]{:S(2)}, u32[]{:S(2)}) collective-permute-start(f32[8,128]{1,0:T(8,128)S(1)} %psum.7), channel_id=1, source_target_pairs={{0,256},{128,384},{256,0},{384,128},{512,768},{640,896},{768,512},... | collective-permute-start | bytes 12296 | tf_op jit(solution)/shard_map/ppermute | solution.py:25
  140.4 9.4 %collective-permute-start.7 = (f32[8,128]{1,0:T(8,128)S(1)}, f32[8,128]{1,0:T(8,128)S(1)}, u32[]{:S(2)}, u32[]{:S(2)}) collective-permute-start(f32[8,128]{1,0:T(8,128)S(1)} %add.301), channel_id=1, source_target_pairs={{0,512},{128,640},{256,768},{384,896},{512,0},{640,128},{768,256},... | collective-permute-start | bytes 12296 | tf_op jit(solution)/shard_map/ppermute | solution.py:25

commit v6 on v5

--- a/solution.py
+++ b/solution.py
@@ -9,7 +9,6 @@
 EXPERT = ("ez", "zp", "x")
 SHARE = ("x", "zp")
 TRADE = ("ez", "x", "zp")
-LANES = 128
 
 
 def three_terms(value):
@@ -118,13 +117,12 @@
     returned = lax.all_to_all(spread.reshape(devices, most, piece), TRADE, 0, 0, tiled=True)
     full_out = returned.reshape(experts, split, most, piece).transpose(0, 2, 1, 3).reshape(experts * most, width)
 
-    loss = jnp.sum(arrived[:, :, piece:].astype(jnp.float32))
-    loss = jnp.broadcast_to(loss, (8, LANES))
+    loss = jnp.sum(arrived[:, :, piece:].astype(jnp.float32), axis=(0, 1))
     loss = add_partner(loss, "dp_0", 1)
     loss = lax.psum(loss, "dp_1")
     loss = add_partner(loss, "dp_0", 2)
     loss = add_partner(loss, "dp_0", 4)
-    z_loss = loss[0, 0] / (n_dp * devices * rows_dev)
+    z_loss = jnp.sum(loss) / (n_dp * devices * rows_dev)
 
     window = logits[:, :experts].T
     peak = jnp.max(jnp.where(member, window, -1e30), axis=0, keepdims=True)

time: 155 us -> 153 us (0.987)
  the two profiles are of different devices: /device:TPU:58 before, /device:TPU:34 now
where the time goes in v6:
time: 153 us; the launch traced here: 152 us
  waiting for transfers between devices  66.2 us (43%)
  starting transfers between devices  62.9 us (41%)
  matrix products  8.91 us (6%)
  local copies, waits for them, and re-layouts  5.52 us (4%)
  between operations  2.98 us (2%)
  other arithmetic  2.75 us (2%)
  blocking collectives  2.45 us (2%)
    all_to_all x1, waiting for transfers between devices, layer(): arrived = lax.all_to_all(outgoing, TRADE, 0, 0, tiled=True)  23.9 us
    all_to_all x1, starting transfers between devices, layer(): arrived = lax.all_to_all(outgoing, TRADE, 0, 0, tiled=True)  22.3 us
    ppermute x1, waiting for transfers between devices, exchange_down(): other = lax.ppermute(other, 'zp', [(i, 1 - i) for i in range(n_zp)])  16.8 us
    ppermute x3, waiting for transfers between devices, add_partner(): lax.ppermute(value, axis, [(i, i ^ bit) for i in range(size)])  13.8 us
    ppermute x3, starting transfers between devices, exchange_down(): part = lax.ppermute(part, 'x', [(i, (i + step) % n_x) for i in range(n_x)])  10.4 us
    all_to_all x2, starting transfers between devices, copy_to(): lax.all_to_all(jnp.broadcast_to(value[None], (count,) + value.shape), axe...  10.4 us
    all_to_all x1, starting transfers between devices, layer(): lax.all_to_all(spread.reshape(devices, most, piece), TRADE, 0, 0, tiled=T...  7.35 us
    ppermute x3, starting transfers between devices, add_partner(): lax.ppermute(value, axis, [(i, i ^ bit) for i in range(size)])  7.26 us
  transfers between devices with their start and end apart: 12, of which 8 were waited for; matrix products, arithmetic and copies ran while one was open for 5% of the time, Pallas kernels for 0%

profile of v6, /device:TPU:34, one launch (start us, length us, event | category | flops | bytes accessed | tf_op | source)
XLA Modules:
  0.0 151.7 jit_solution(10436439516787293027)
XLA Ops:
  1.9 1.8 %fusion.58 = (f32[128]{0:T(128)S(1)}, f32[128,128]{0,1:T(8,128)S(1)}) fusion(bf16[4096,128]{1,0:T(8,128)(2,1)} %param.7, bf16[1,128,4096]{2,1,0:T(8,128)(2,1)S(1)} %copy-done), kind=kOutput, calls=%fused_computation.120 | convolution fusion | flops 134233984 | bytes 2163200 | tf_op jit(solution)/shard_map/dot_general | solution.py:76
  5.5 22.3 %all-to-all-start = ((bf16[64,4,640]{2,1,0:T(4,128)(2,1)}), bf16[64,4,640]{2,1,0:T(4,128)(2,1)S(1)}, u32[]{:S(2)}, u32[]{:S(2)}) async-start(bf16[64,4,640]{2,1,0:T(4,128)(2,1)} %copy.26), calls=%async_computation | async-start | bytes 655360 | tf_op jit(solution)/shard_map/all_to_all | solution.py:84
  28.3 23.9 %all-to-all-done = bf16[64,4,640]{2,1,0:T(4,128)(2,1)S(1)} async-done(((bf16[64,4,640]{2,1,0:T(4,128)(2,1)}), bf16[64,4,640]{2,1,0:T(4,128)(2,1)S(1)}, u32[]{:S(2)}, u32[]{:S(2)}) %all-to-all-start) | async-done | bytes 327712 | tf_op jit(solution)/shard_map/all_to_all | solution.py:84
  53.6 5.1 %all-to-all-start.1 = ((bf16[8,128,512]{2,1,0:T(8,128)(2,1)}), bf16[8,128,512]{2,1,0:T(8,128)(2,1)}, u32[]{:S(2)}, u32[]{:S(2)}) async-start(bf16[8,128,512]{2,1,0:T(8,128)(2,1)} %broadcast_in_dim.86), calls=%async_computation.1 | async-start | bytes 2097152 | tf_op jit(solution)/shard_map/all_to_all | solution.py:51
  58.8 3.4 %collective-permute-start = (bf16[192,1024]{1,0:T(8,128)(2,1)S(1)}, bf16[192,1024]{1,0:T(8,128)(2,1)}, u32[]{:S(2)}, u32[]{:S(2)}) collective-permute-start(bf16[192,1024]{1,0:T(8,128)(2,1)S(1)} %pad_maximum_fusion), channel_id=1, source_target_pairs={{0,4},{4,0},{1,5},{5,1},{2,6},{6,2},{3,7},{7,3},{8,12},{12,8},{9,1... | collective-permute-start | bytes 1179656 | tf_op jit(solution)/shard_map/ppermute | solution.py:36
  62.3 16.8 %collective-permute-done = bf16[192,1024]{1,0:T(8,128)(2,1)} collective-permute-done((bf16[192,1024]{1,0:T(8,128)(2,1)S(1)}, bf16[192,1024]{1,0:T(8,128)(2,1)}, u32[]{:S(2)}, u32[]{:S(2)}) %collective-permute-start) | collective-permute-done | bytes 393248 | tf_op jit(solution)/shard_map/ppermute | solution.py:36
  80.4 3.4 %collective-permute-start.1 = (bf16[2,192,256]{2,1,0:T(8,128)(2,1)S(1)}, bf16[2,192,256]{2,1,0:T(8,128)(2,1)S(1)}, u32[]{:S(2)}, u32[]{:S(2)}) collective-permute-start(bf16[2,192,256]{2,1,0:T(8,128)(2,1)S(1)} %pad_maximum_fusion.2), channel_id=1, source_target_pairs={{0,1},{1,2},{2,3},{3,0},{4,5},{5,6},{6,7},{7,4},{8,9},{9,10},{10,1... | collective-permute-start | bytes 589832 | tf_op jit(solution)/shard_map/ppermute | solution.py:44
  83.8 3.0 %collective-permute-start.2 = (bf16[2,192,256]{2,1,0:T(8,128)(2,1)S(1)}, bf16[2,192,256]{2,1,0:T(8,128)(2,1)S(1)}, u32[]{:S(2)}, u32[]{:S(2)}) collective-permute-start(bf16[2,192,256]{2,1,0:T(8,128)(2,1)S(1)} %pad_maximum_fusion.3), channel_id=1, source_target_pairs={{0,2},{1,3},{2,0},{3,1},{4,6},{5,7},{6,4},{7,5},{8,10},{9,11},{10,... | collective-permute-start | bytes 589832 | tf_op jit(solution)/shard_map/ppermute | solution.py:44
  86.9 4.0 %collective-permute-start.3 = (bf16[2,192,256]{2,1,0:T(8,128)(2,1)S(1)}, bf16[2,192,256]{2,1,0:T(8,128)(2,1)S(1)}, u32[]{:S(2)}, u32[]{:S(2)}) collective-permute-start(bf16[2,192,256]{2,1,0:T(8,128)(2,1)S(1)} %pad_maximum_fusion.4), channel_id=1, source_target_pairs={{0,3},{1,0},{2,1},{3,2},{4,7},{5,4},{6,5},{7,6},{8,11},{9,8},{10,9... | collective-permute-start | bytes 589832 | tf_op jit(solution)/shard_map/ppermute | solution.py:44
  91.0 2.5 %collective-permute-done.2 = bf16[2,192,256]{2,1,0:T(8,128)(2,1)S(1)} collective-permute-done((bf16[2,192,256]{2,1,0:T(8,128)(2,1)S(1)}, bf16[2,192,256]{2,1,0:T(8,128)(2,1)S(1)}, u32[]{:S(2)}, u32[]{:S(2)}) %collective-permute-start.2) | collective-permute-done | bytes 196640 | tf_op jit(solution)/shard_map/ppermute | solution.py:44
  93.5 2.0 %collective-permute-done.3 = bf16[2,192,256]{2,1,0:T(8,128)(2,1)S(1)} collective-permute-done((bf16[2,192,256]{2,1,0:T(8,128)(2,1)S(1)}, bf16[2,192,256]{2,1,0:T(8,128)(2,1)S(1)}, u32[]{:S(2)}, u32[]{:S(2)}) %collective-permute-start.3) | collective-permute-done | bytes 196640 | tf_op jit(solution)/shard_map/ppermute | solution.py:44
  95.5 1.9 %collective-permute-start.4 = (bf16[8,192,256]{2,1,0:T(8,128)(2,1)S(1)}, bf16[8,192,256]{2,1,0:T(8,128)(2,1)S(1)}, u32[]{:S(2)}, u32[]{:S(2)}) collective-permute-start(bf16[8,192,256]{2,1,0:T(8,128)(2,1)S(1)} %constant_dynamic-update-slice_fusion), channel_id=1, source_target_pairs={{0,64},{64,0},{1,65},{65,1},{2,66},{66,2},{3,67},{67,3},{4,68},{68... | collective-permute-start | bytes 2359304 | tf_op jit(solution)/shard_map/ppermute | solution.py:46
  97.4 2.4 %fusion.9 = f32[128,192]{0,1:T(8,128)S(1)} fusion(bf16[8,128,512]{2,1,0:T(8,128)(2,1)} %all-to-all-done.1, bf16[24,8,8,512]{3,2,1,0:T(8,128)(2,1)} %bitcast.127), kind=kOutput, calls=%fused_computation.15 | convolution fusion | flops 201326592 | bytes 2719744 | tf_op jit(solution)/shard_map/kpd,kdf->pf/dot_general | solution.py:103
  99.9 1.8 %fusion.18 = bf16[128,192]{0,1:T(8,128)(2,1)S(1)} fusion(bf16[8,128,512]{2,1,0:T(8,128)(2,1)} %all-to-all-done.1, bf16[24,8,8,512]{3,2,1,0:T(8,128)(2,1)S(1)} %bitcast.128, f32[128,192]{0,1:T(8,128)S(1)} %fusion.9), kind=kOutput, calls=%fused_computation.18 | convolution fusion | flops 201474048 | bytes 2768896 | tf_op jit(solution)/shard_map/kpd,kdf->pf/dot_general | solution.py:104
  102.5 5.2 %all-to-all-start.2 = ((bf16[8,128,192]{1,2,0:T(8,128)(2,1)}), bf16[8,128,192]{1,2,0:T(8,128)(2,1)S(1)}, u32[]{:S(2)}, u32[]{:S(2)}) async-start(bf16[8,128,192]{1,2,0:T(8,128)(2,1)} %broadcast_in_dim.88), calls=%async_computation.2 | async-start | bytes 786432 | tf_op jit(solution)/shard_map/all_to_all | solution.py:51
  107.8 7.2 %all-to-all-done.2 = bf16[8,128,192]{1,2,0:T(8,128)(2,1)S(1)} async-done(((bf16[8,128,192]{1,2,0:T(8,128)(2,1)}), bf16[8,128,192]{1,2,0:T(8,128)(2,1)S(1)}, u32[]{:S(2)}, u32[]{:S(2)}) %all-to-all-start.2) | async-done | bytes 393248 | tf_op jit(solution)/shard_map/all_to_all | solution.py:51
  116.6 7.3 %all-to-all-start.3 = ((bf16[64,4,512]{2,1,0:T(4,128)(2,1)}), bf16[64,4,512]{2,1,0:T(4,128)(2,1)S(1)}, u32[]{:S(2)}, u32[]{:S(2)}) async-start(bf16[64,4,512]{2,1,0:T(4,128)(2,1)} %reshape.263), calls=%async_computation.3 | async-start | bytes 524288 | tf_op jit(solution)/shard_map/all_to_all | solution.py:117
  124.1 2.6 %collective-permute-start.5 = (f32[128]{0:T(128)S(1)}, f32[128]{0:T(128)S(1)}, u32[]{:S(2)}, u32[]{:S(2)}) collective-permute-start(f32[128]{0:T(128)S(1)} %convert_reduce_fusion), channel_id=1, source_target_pairs={{0,128},{128,0},{256,384},{384,256},{512,640},{640,512},{768,896},... | collective-permute-start | bytes 1544 | tf_op jit(solution)/shard_map/ppermute | solution.py:24
  126.7 2.9 %collective-permute-done.5 = f32[128]{0:T(128)S(1)} collective-permute-done((f32[128]{0:T(128)S(1)}, f32[128]{0:T(128)S(1)}, u32[]{:S(2)}, u32[]{:S(2)}) %collective-permute-start.5) | collective-permute-done | bytes 544 | tf_op jit(solution)/shard_map/ppermute | solution.py:24
  129.6 2.4 %psum.7 = f32[128]{0:T(128)S(1)} all-reduce(f32[128]{0:T(128)S(1)} %add.300), channel_id=1, replica_groups=mesh['dp_0'=8,'dp_1'=2,'ez'=8,'zp'=2,'x'=4] {'dp_1'}, use_global_device_ids=true, to_apply=%region_9.10 | all-reduce | flops 128 | bytes 1024 | tf_op jit(solution)/shard_map/psum | solution.py:122
  132.0 2.7 %collective-permute-start.6 = (f32[128]{0:T(128)S(1)}, f32[128]{0:T(128)S(1)}, u32[]{:S(2)}, u32[]{:S(2)}) collective-permute-start(f32[128]{0:T(128)S(1)} %psum.7), channel_id=1, source_target_pairs={{0,256},{128,384},{256,0},{384,128},{512,768},{640,896},{768,512},... | collective-permute-start | bytes 1544 | tf_op jit(solution)/shard_map/ppermute | solution.py:24
  134.7 3.6 %collective-permute-done.6 = f32[128]{0:T(128)S(1)} collective-permute-done((f32[128]{0:T(128)S(1)}, f32[128]{0:T(128)S(1)}, u32[]{:S(2)}, u32[]{:S(2)}) %collective-permute-start.6) | collective-permute-done | bytes 544 | tf_op jit(solution)/shard_map/ppermute | solution.py:24
  138.4 2.0 %collective-permute-start.7 = (f32[128]{0:T(128)S(1)}, f32[128]{0:T(128)S(1)}, u32[]{:S(2)}, u32[]{:S(2)}) collective-permute-start(f32[128]{0:T(128)S(1)} %add.301), channel_id=1, source_target_pairs={{0,512},{128,640},{256,768},{384,896},{512,0},{640,128},{768,256},... | collective-permute-start | bytes 1544 | tf_op jit(solution)/shard_map/ppermute | solution.py:24
  140.4 7.3 %collective-permute-done.7 = f32[128]{0:T(128)S(1)} collective-permute-done((f32[128]{0:T(128)S(1)}, f32[128]{0:T(128)S(1)}, u32[]{:S(2)}, u32[]{:S(2)}) %collective-permute-start.7) | collective-permute-done | bytes 544 | tf_op jit(solution)/shard_map/ppermute | solution.py:24
  (67 shorter events, 11.2 us)
Async XLA Ops:
  0.6 1.2 copy-start
  0.6 3.1 %copy-start.2 = (s32[1,8,128]{2,1,0:T(8,128)S(1)}, s32[1,8,128]{2,1,0:T(8,128)}, u32[]{:S(2)}) copy-start(s32[1,8,128]{2,1,0:T(8,128)} %param.8) | copy-start | bytes 12292
  5.5 46.6 %all-to-all-start = ((bf16[64,4,640]{2,1,0:T(4,128)(2,1)}), bf16[64,4,640]{2,1,0:T(4,128)(2,1)S(1)}, u32[]{:S(2)}, u32[]{:S(2)}) async-start(bf16[64,4,640]{2,1,0:T(4,128)(2,1)} %copy.26), calls=%async_computation | async-start | bytes 655360 | tf_op jit(solution)/shard_map/all_to_all | solution.py:84
  52.5 6.2 %copy-start.1 = (bf16[192,4096]{1,0:T(8,128)(2,1)S(1)}, bf16[192,4096]{1,0:T(8,128)(2,1)}, u32[]{:S(2)}) copy-start(bf16[192,4096]{1,0:T(8,128)(2,1)} %param.11) | copy-start | bytes 4718596
  53.6 43.8 %all-to-all-start.1 = ((bf16[8,128,512]{2,1,0:T(8,128)(2,1)}), bf16[8,128,512]{2,1,0:T(8,128)(2,1)}, u32[]{:S(2)}, u32[]{:S(2)}) async-start(bf16[8,128,512]{2,1,0:T(8,128)(2,1)} %broadcast_in_dim.86), calls=%async_computation.1 | async-start | bytes 2097152 | tf_op jit(solution)/shard_map/all_to_all | solution.py:51
  58.8 20.3 %collective-permute-start = (bf16[192,1024]{1,0:T(8,128)(2,1)S(1)}, bf16[192,1024]{1,0:T(8,128)(2,1)}, u32[]{:S(2)}, u32[]{:S(2)}) collective-permute-start(bf16[192,1024]{1,0:T(8,128)(2,1)S(1)} %pad_maximum_fusion), channel_id=1, source_target_pairs={{0,4},{4,0},{1,5},{5,1},{2,6},{6,2},{3,7},{7,3},{8,12},{12,8},{9,1... | collective-permute-start | bytes 1179656 | tf_op jit(solution)/shard_map/ppermute | solution.py:36
  80.4 10.6 %collective-permute-start.1 = (bf16[2,192,256]{2,1,0:T(8,128)(2,1)S(1)}, bf16[2,192,256]{2,1,0:T(8,128)(2,1)S(1)}, u32[]{:S(2)}, u32[]{:S(2)}) collective-permute-start(bf16[2,192,256]{2,1,0:T(8,128)(2,1)S(1)} %pad_maximum_fusion.2), channel_id=1, source_target_pairs={{0,1},{1,2},{2,3},{3,0},{4,5},{5,6},{6,7},{7,4},{8,9},{9,10},{10,1... | collective-permute-start | bytes 589832 | tf_op jit(solution)/shard_map/ppermute | solution.py:44
  83.8 9.6 %collective-permute-start.2 = (bf16[2,192,256]{2,1,0:T(8,128)(2,1)S(1)}, bf16[2,192,256]{2,1,0:T(8,128)(2,1)S(1)}, u32[]{:S(2)}, u32[]{:S(2)}) collective-permute-start(bf16[2,192,256]{2,1,0:T(8,128)(2,1)S(1)} %pad_maximum_fusion.3), channel_id=1, source_target_pairs={{0,2},{1,3},{2,0},{3,1},{4,6},{5,7},{6,4},{7,5},{8,10},{9,11},{10,... | collective-permute-start | bytes 589832 | tf_op jit(solution)/shard_map/ppermute | solution.py:44
  86.9 8.6 %collective-permute-start.3 = (bf16[2,192,256]{2,1,0:T(8,128)(2,1)S(1)}, bf16[2,192,256]{2,1,0:T(8,128)(2,1)S(1)}, u32[]{:S(2)}, u32[]{:S(2)}) collective-permute-start(bf16[2,192,256]{2,1,0:T(8,128)(2,1)S(1)} %pad_maximum_fusion.4), channel_id=1, source_target_pairs={{0,3},{1,0},{2,1},{3,2},{4,7},{5,4},{6,5},{7,6},{8,11},{9,8},{10,9... | collective-permute-start | bytes 589832 | tf_op jit(solution)/shard_map/ppermute | solution.py:44
  95.5 6.2 %collective-permute-start.4 = (bf16[8,192,256]{2,1,0:T(8,128)(2,1)S(1)}, bf16[8,192,256]{2,1,0:T(8,128)(2,1)S(1)}, u32[]{:S(2)}, u32[]{:S(2)}) collective-permute-start(bf16[8,192,256]{2,1,0:T(8,128)(2,1)S(1)} %constant_dynamic-update-slice_fusion), channel_id=1, source_target_pairs={{0,64},{64,0},{1,65},{65,1},{2,66},{66,2},{3,67},{67,3},{4,68},{68... | collective-permute-start | bytes 2359304 | tf_op jit(solution)/shard_map/ppermute | solution.py:46
  97.4 2.4 %copy-start.3 = (bf16[4096,192]{0,1:T(8,128)(2,1)S(1)}, bf16[4096,192]{0,1:T(8,128)(2,1)}, u32[]{:S(2)}) copy-start(bf16[4096,192]{0,1:T(8,128)(2,1)} %param.10) | copy-start | bytes 4718596
  102.5 12.4 %all-to-all-start.2 = ((bf16[8,128,192]{1,2,0:T(8,128)(2,1)}), bf16[8,128,192]{1,2,0:T(8,128)(2,1)S(1)}, u32[]{:S(2)}, u32[]{:S(2)}) async-start(bf16[8,128,192]{1,2,0:T(8,128)(2,1)} %broadcast_in_dim.88), calls=%async_computation.2 | async-start | bytes 786432 | tf_op jit(solution)/shard_map/all_to_all | solution.py:51
  116.6 32.3 %all-to-all-start.3 = ((bf16[64,4,512]{2,1,0:T(4,128)(2,1)}), bf16[64,4,512]{2,1,0:T(4,128)(2,1)S(1)}, u32[]{:S(2)}, u32[]{:S(2)}) async-start(bf16[64,4,512]{2,1,0:T(4,128)(2,1)} %reshape.263), calls=%async_computation.3 | async-start | bytes 524288 | tf_op jit(solution)/shard_map/all_to_all | solution.py:117
  124.1 5.5 %collective-permute-start.5 = (f32[128]{0:T(128)S(1)}, f32[128]{0:T(128)S(1)}, u32[]{:S(2)}, u32[]{:S(2)}) collective-permute-start(f32[128]{0:T(128)S(1)} %convert_reduce_fusion), channel_id=1, source_target_pairs={{0,128},{128,0},{256,384},{384,256},{512,640},{640,512},{768,896},... | collective-permute-start | bytes 1544 | tf_op jit(solution)/shard_map/ppermute | solution.py:24
  132.0 6.3 %collective-permute-start.6 = (f32[128]{0:T(128)S(1)}, f32[128]{0:T(128)S(1)}, u32[]{:S(2)}, u32[]{:S(2)}) collective-permute-start(f32[128]{0:T(128)S(1)} %psum.7), channel_id=1, source_target_pairs={{0,256},{128,384},{256,0},{384,128},{512,768},{640,896},{768,512},... | collective-permute-start | bytes 1544 | tf_op jit(solution)/shard_map/ppermute | solution.py:24
  138.4 9.4 %collective-permute-start.7 = (f32[128]{0:T(128)S(1)}, f32[128]{0:T(128)S(1)}, u32[]{:S(2)}, u32[]{:S(2)}) collective-permute-start(f32[128]{0:T(128)S(1)} %add.301), channel_id=1, source_target_pairs={{0,512},{128,640},{256,768},{384,896},{512,0},{640,128},{768,256},... | collective-permute-start | bytes 1544 | tf_op jit(solution)/shard_map/ppermute | solution.py:24
